TPU v7x, 32 devices: a whole 2x2x4 slice. The times are simulated.
32 devices in a mesh: dp: 2 (over y), row: 4 (over z), col: 4 (over x, core).
Axes of the slice: x: 2, y: 2, z: 4, core: 2. Of those that a mesh axis runs over, the one named last changes fastest.
Arguments:
- hidden: bfloat16 [16384, 768], P(('dp', 'row', 'col')), may hold values from -6 to 6
- segments: int32 [16, 1024], P(('dp', 'row')), may hold values from 0 to 7, never falling along the last dimension, each value on 1 to 800 neighbouring positions
- query_weight: bfloat16 [768, 768], P('row', 'col'), may hold values from -0.21875 to 0.21875
- key_weight: bfloat16 [768, 768], P('row', 'col'), may hold values from -0.21875 to 0.21875
- value_weight: bfloat16 [768, 768], P('row', 'col'), may hold values from -0.21875 to 0.21875
- query_bias: float32 [768], P('col'), may hold values from -3 to 3
- value_bias: float32 [768], P('col'), may hold values from -3 to 3
- output_weight: bfloat16 [768, 768], P('row', 'col'), may hold values from -1.75 to 1.75
- output_bias: float32 [768], replicated, may hold values from -3 to 3
- first_gain: float32 [768], replicated, may hold values from 0.25 to 1.75
- first_shift: float32 [768], replicated, may hold values from -3 to 3
- inner_weight: bfloat16 [768, 3072], P('row', 'col'), may hold values from -0.21875 to 0.21875
- inner_bias: float32 [3072], P('col'), may hold values from -3 to 3
- outer_weight: bfloat16 [768, 3072], P('row', 'col'), may hold values from -0.15625 to 0.15625
- outer_bias: float32 [768], replicated, may hold values from -3 to 3
- second_gain: float32 [768], replicated, may hold values from 0.25 to 1.75
- second_shift: float32 [768], replicated, may hold values from -3 to 3
- upstream: bfloat16 [16384, 768], P(('dp', 'row', 'col')), may hold values from -6 to 6
Outputs:
- layer_out: bfloat16 [16384, 768], P(('dp', 'row', 'col'))
- grad_inputs: float32 [16384, 768], P(('dp', 'row', 'col'))
- grad_query: float32 [768, 768], P('row', 'col')
- grad_key: float32 [768, 768], P('row', 'col')
- grad_value: float32 [768, 768], P('row', 'col')
- grad_query_bias: float32 [768], P('col')
- grad_value_bias: float32 [768], P('col')
- grad_output: float32 [768, 768], P('row', 'col')
- grad_output_bias: float32 [768], replicated
- grad_gain_one: float32 [768], replicated
- grad_shift_one: float32 [768], replicated
- grad_inner: float32 [768, 3072], P('row', 'col')
- grad_inner_bias: float32 [3072], P('col')
- grad_outer: float32 [768, 3072], P('row', 'col')
- grad_outer_bias: float32 [768], replicated
- grad_gain_two: float32 [768], replicated
- grad_shift_two: float32 [768], replicated
Inputs may be any that keep to these rules, and one draw needn't show every extreme that they name: `segments`: segment numbers never fall along a sequence; each document holds 1 to 800 tokens, and one of each sequence holds exactly 800.
All inputs are finite; a program needn't handle non-finite values.
Results may differ from a plain program's by a relative error of at most 0.02.
Values may be sent and summed in bfloat16 or wider, within the bound.
A program may use at most 128 MiB of HBM per device.

v0:
```python
import jax
import jax.numpy as jnp
from jax import lax
from jax.sharding import PartitionSpec as P

HEAD_DIM = 64


EPS_NORM = 1e-12
NEG_FILL = -1e30


def gelu_exact(values):
    return jax.nn.gelu(values, approximate=False)


def gather_tokens(acts):
    return lax.all_gather(acts, "col", axis=0, tiled=True)


def gather_grads(grads):
    return lax.all_gather(grads, "col", axis=0, tiled=True)


def leave_branch(acts, weight_full, bias):
    partial_sum = jnp.einsum("tc,dc->td", acts, weight_full, preferred_element_type=jnp.float32)
    return lax.psum_scatter(partial_sum, "col", scatter_dimension=0, tiled=True) + bias


def back_to_tokens(grads, weight_full):
    partial_sum = jnp.einsum("tf,df->td", grads, weight_full, preferred_element_type=jnp.float32)
    return lax.psum_scatter(
        partial_sum.astype(jnp.bfloat16), "col", scatter_dimension=0, tiled=True
    ).astype(jnp.float32)


def norm_forward(values, gain, shift):
    means = jnp.mean(values, axis=1, keepdims=True)
    centered = values - means
    variance = jnp.mean(centered * centered, axis=1, keepdims=True)
    inv_scale = lax.rsqrt(variance + EPS_NORM)
    normed = centered * inv_scale
    return (normed, inv_scale, normed * gain + shift)


def norm_backward(grads, normed, inv_scale, gain):
    scaled = grads * gain
    mean_plain = jnp.mean(scaled, axis=1, keepdims=True)
    mean_normed = jnp.mean(scaled * normed, axis=1, keepdims=True)
    grad_in = inv_scale * (scaled - mean_plain - normed * mean_normed)
    return (grad_in, jnp.sum(grads * normed, axis=0), jnp.sum(grads, axis=0))


def masked_scores(query, keys, segment):
    length = query.shape[0]
    heads = query.shape[1] // HEAD_DIM
    query_heads = query.reshape(length, heads, HEAD_DIM)
    key_heads = keys.reshape(length, heads, HEAD_DIM)
    scores = jnp.einsum(
        "qhd,khd->hqk", query_heads, key_heads, preferred_element_type=jnp.float32
    ) * HEAD_DIM ** (-0.5)
    same_doc = segment[:, None] == segment[None, :]
    return (query_heads, key_heads, jnp.where(same_doc[None], scores, NEG_FILL))


def attend_forward(item):
    query, keys, values, segment = item
    length = query.shape[0]
    heads = query.shape[1] // HEAD_DIM
    query_heads, key_heads, scores = masked_scores(query, keys, segment)
    peak = jnp.max(scores, axis=2, keepdims=True)
    expos = jnp.exp(scores - peak)
    totals = jnp.sum(expos, axis=2, keepdims=True)
    probs = (expos / totals).astype(jnp.bfloat16)
    value_heads = values.reshape(length, heads, HEAD_DIM)
    mixed = jnp.einsum("hqk,khd->qhd", probs, value_heads, preferred_element_type=jnp.float32)
    return (mixed.reshape(length, heads * HEAD_DIM), (peak + jnp.log(totals))[:, :, 0])


def attend_backward(item):
    query, keys, values, segment, logsum, grad_mixed = item
    length = query.shape[0]
    heads = query.shape[1] // HEAD_DIM
    query_heads, key_heads, scores = masked_scores(query, keys, segment)
    probs = jnp.exp(scores - logsum[:, :, None])
    value_heads = values.reshape(length, heads, HEAD_DIM)
    grad_heads = grad_mixed.reshape(length, heads, HEAD_DIM)
    value_rows = jnp.einsum(
        "hqk,qhd->khd", probs.astype(jnp.bfloat16), grad_heads, preferred_element_type=jnp.float32
    )
    grad_probs = jnp.einsum(
        "qhd,khd->hqk", grad_heads, value_heads, preferred_element_type=jnp.float32
    )
    inner_sum = jnp.sum(probs * grad_probs, axis=2, keepdims=True)
    grad_scores = (probs * (grad_probs - inner_sum)).astype(jnp.bfloat16)
    query_rows = jnp.einsum(
        "hqk,khd->qhd", grad_scores, key_heads, preferred_element_type=jnp.float32
    ) * HEAD_DIM ** (-0.5)
    key_rows = jnp.einsum(
        "hqk,qhd->khd", grad_scores, query_heads, preferred_element_type=jnp.float32
    ) * HEAD_DIM ** (-0.5)
    width = heads * HEAD_DIM
    joined = jnp.concatenate(
        [
            query_rows.reshape(length, width),
            key_rows.reshape(length, width),
            value_rows.reshape(length, width),
        ],
        axis=1,
    )
    return joined.astype(jnp.bfloat16)


def shards(
    hidden,
    segments,
    query_weight,
    key_weight,
    value_weight,
    query_bias,
    value_bias,
    output_weight,
    output_bias,
    first_gain,
    first_shift,
    inner_weight,
    inner_bias,
    outer_weight,
    outer_bias,
    second_gain,
    second_shift,
    upstream,
):
    width_local = query_weight.shape[1]
    seq_count = segments.shape[0]
    seq_len = segments.shape[1]
    joint_shard = jnp.concatenate([query_weight, key_weight, value_weight], axis=1)
    joint_bias = jnp.concatenate([query_bias, jnp.zeros_like(query_bias), value_bias])
    joint_full, output_full, inner_full, outer_full = (
        lax.all_gather(joint_shard, "row", axis=0, tiled=True),
        lax.all_gather(output_weight, "row", axis=0, tiled=True),
        lax.all_gather(inner_weight, "row", axis=0, tiled=True),
        lax.all_gather(outer_weight, "row", axis=0, tiled=True),
    )

    def by_sequence(block):
        return block.reshape(seq_count, seq_len, width_local)

    hidden_rows = gather_tokens(hidden)
    joint = (
        jnp.dot(hidden_rows, joint_full, preferred_element_type=jnp.float32) + joint_bias
    ).astype(jnp.bfloat16)
    query = by_sequence(joint[:, :width_local])
    keys = by_sequence(joint[:, width_local : 2 * width_local])
    values = by_sequence(joint[:, 2 * width_local :])
    mixed, logsum = lax.map(attend_forward, (query, keys, values, segments))
    mixed = mixed.reshape(seq_count * seq_len, width_local).astype(jnp.bfloat16)
    branch = leave_branch(mixed, output_full, output_bias)
    first_normed, first_scale, first_out = norm_forward(
        hidden.astype(jnp.float32) + branch, first_gain, first_shift
    )
    first_rows = gather_tokens(first_out.astype(jnp.bfloat16))
    inner_pre = jnp.dot(first_rows, inner_full, preferred_element_type=jnp.float32) + inner_bias
    activated, gelu_pull = jax.vjp(gelu_exact, inner_pre)
    activated = activated.astype(jnp.bfloat16)
    outer_branch = leave_branch(activated, outer_full, outer_bias)
    second_normed, second_scale, layer_out = norm_forward(
        first_out + outer_branch, second_gain, second_shift
    )
    joint_full, output_full, inner_full, outer_full = (
        lax.all_gather(joint_shard, "row", axis=0, tiled=True),
        lax.all_gather(output_weight, "row", axis=0, tiled=True),
        lax.all_gather(inner_weight, "row", axis=0, tiled=True),
        lax.all_gather(outer_weight, "row", axis=0, tiled=True),
    )
    grad_second, grad_gain_two, grad_shift_two = norm_backward(
        upstream.astype(jnp.float32), second_normed, second_scale, second_gain
    )
    grad_branch_two = grad_second.astype(jnp.bfloat16)
    grad_outer_bias = jnp.sum(grad_branch_two, axis=0, dtype=jnp.float32)
    outer_rows = gather_grads(grad_branch_two)
    grad_active = jnp.dot(outer_rows, outer_full, preferred_element_type=jnp.float32)
    grad_outer = jnp.einsum("td,tf->df", outer_rows, activated, preferred_element_type=jnp.float32)
    grad_inner_pre = gelu_pull(grad_active)[0].astype(jnp.bfloat16)
    grad_inner = jnp.einsum(
        "td,tf->df", first_rows, grad_inner_pre, preferred_element_type=jnp.float32
    )
    grad_inner_bias = jnp.sum(grad_inner_pre, axis=0, dtype=jnp.float32)
    first_part = back_to_tokens(grad_inner_pre, inner_full)
    grad_first = first_part + grad_second
    grad_sum_one, grad_gain_one, grad_shift_one = norm_backward(
        grad_first, first_normed, first_scale, first_gain
    )
    grad_branch_one = grad_sum_one.astype(jnp.bfloat16)
    grad_output_bias = jnp.sum(grad_branch_one, axis=0, dtype=jnp.float32)
    branch_rows = gather_grads(grad_branch_one)
    grad_mixed = jnp.dot(branch_rows, output_full, preferred_element_type=jnp.float32).astype(
        jnp.bfloat16
    )
    grad_output = jnp.einsum("td,tc->dc", branch_rows, mixed, preferred_element_type=jnp.float32)
    grad_joint = lax.map(
        attend_backward, (query, keys, values, segments, logsum, by_sequence(grad_mixed))
    )
    grad_joint = grad_joint.reshape(seq_count * seq_len, 3 * width_local)
    grad_joint_weight = jnp.einsum(
        "td,tf->df", hidden_rows, grad_joint, preferred_element_type=jnp.float32
    )
    grad_joint_bias = jnp.sum(grad_joint, axis=0, dtype=jnp.float32)
    input_part = back_to_tokens(grad_joint, joint_full)
    grad_inputs = input_part + grad_sum_one
    weight_grads = (
        lax.psum_scatter(
            grad_joint_weight.astype(jnp.bfloat16), "row", scatter_dimension=0, tiled=True
        ).astype(jnp.float32),
        lax.psum_scatter(
            grad_output.astype(jnp.bfloat16), "row", scatter_dimension=0, tiled=True
        ).astype(jnp.float32),
        lax.psum_scatter(
            grad_inner.astype(jnp.bfloat16), "row", scatter_dimension=0, tiled=True
        ).astype(jnp.float32),
        lax.psum_scatter(
            grad_outer.astype(jnp.bfloat16), "row", scatter_dimension=0, tiled=True
        ).astype(jnp.float32),
    )
    weight_grads = (
        lax.psum(weight_grads[0].astype(jnp.bfloat16), "dp").astype(jnp.float32),
        lax.psum(weight_grads[1].astype(jnp.bfloat16), "dp").astype(jnp.float32),
        lax.psum(weight_grads[2].astype(jnp.bfloat16), "dp").astype(jnp.float32),
        lax.psum(weight_grads[3].astype(jnp.bfloat16), "dp").astype(jnp.float32),
    )
    grad_joint_weight, grad_output, grad_inner, grad_outer = weight_grads
    grad_joint_bias, grad_inner_bias = lax.psum((grad_joint_bias, grad_inner_bias), ("dp", "row"))
    (
        grad_output_bias,
        grad_gain_one,
        grad_shift_one,
        grad_outer_bias,
        grad_gain_two,
        grad_shift_two,
    ) = lax.psum(
        (
            grad_output_bias,
            grad_gain_one,
            grad_shift_one,
            grad_outer_bias,
            grad_gain_two,
            grad_shift_two,
        ),
        ("dp", "row", "col"),
    )
    grad_query = grad_joint_weight[:, :width_local]
    grad_key = grad_joint_weight[:, width_local : 2 * width_local]
    grad_value = grad_joint_weight[:, 2 * width_local :]
    grad_query_bias = grad_joint_bias[:width_local]
    grad_value_bias = grad_joint_bias[2 * width_local :]
    return (
        layer_out.astype(jnp.bfloat16),
        grad_inputs,
        grad_query,
        grad_key,
        grad_value,
        grad_query_bias,
        grad_value_bias,
        grad_output,
        grad_output_bias,
        grad_gain_one,
        grad_shift_one,
        grad_inner,
        grad_inner_bias,
        grad_outer,
        grad_outer_bias,
        grad_gain_two,
        grad_shift_two,
    )


def solution(mesh):
    in_specs = (
        P(("dp", "row", "col"), None),
        P(("dp", "row"), None),
        P("row", "col"),
        P("row", "col"),
        P("row", "col"),
        P("col"),
        P("col"),
        P("row", "col"),
        P(),
        P(),
        P(),
        P("row", "col"),
        P("col"),
        P("row", "col"),
        P(),
        P(),
        P(),
        P(("dp", "row", "col"), None),
    )
    out_specs = (
        P(("dp", "row", "col"), None),
        P(("dp", "row", "col"), None),
        P("row", "col"),
        P("row", "col"),
        P("row", "col"),
        P("col"),
        P("col"),
        P("row", "col"),
        P(),
        P(),
        P(),
        P("row", "col"),
        P("col"),
        P("row", "col"),
        P(),
        P(),
        P(),
    )
    return jax.shard_map(shards, mesh=mesh, in_specs=in_specs, out_specs=out_specs, check_vma=False)
```

profile of v0, /device:TPU:0, one launch (start us, length us, event | category | flops | bytes accessed | tf_op | source)
XLA Modules:
  0.0 668.6 jit_solution(4088758631724754869)
XLA Ops:
  8.8 18.2 %all_gather.30 = bf16[768,192]{1,0:T(8,128)(2,1)} all-gather(bf16[192,192]{1,0:T(8,128)(2,1)} %param.29), channel_id=1, replica_groups=mesh['dp'=2,'row'=4,'col'=4] {'row'}, dimensions={0}, use_global_device_ids=true | all-gather | bytes 368640 | tf_op jit(solution)/shard_map/all_gather | solution.py:141
  28.9 19.6 %all_gather.28 = bf16[768,576]{1,0:T(8,128)(2,1)S(1)} all-gather(bf16[192,576]{1,0:T(8,128)(2,1)S(1)} %pad_maximum_fusion), channel_id=1, replica_groups=mesh['dp'=2,'row'=4,'col'=4] {'row'}, dimensions={0}, use_global_device_ids=true | all-gather | bytes 1105920 | tf_op jit(solution)/shard_map/all_gather | solution.py:140
  48.5 4.7 fusion.22
  55.6 31.1 %while.22 = (s32[]{:T(128)}, bf16[2,1024,192]{1,2,0:T(8,128)(2,1)}, f32[2,3,1024]{2,1,0:T(4,128)S(1)}, bf16[2,1024,192]{1,2,0:T(8,128)(2,1)}, s32[2,1024]{1,0:T(...) while((s32[]{:T(128)}, bf16[2,1024,192]{1,2,0:T(8,128)(2,1)}, ...), condition=%wide.region_3.4_spmd, body=%wide.region_0.3_spmd.sunk | while | flops 844100608 | bytes 57270468 | solution.py:156
  58.5 2.8 fusion.102
  61.4 3.9 fusion.103
  65.2 5.0 fusion.104
  74.1 2.8 fusion.102
  76.9 3.9 fusion.103
  80.8 5.0 fusion.104
  88.9 4.7 fusion.41
  94.3 58.2 %reduce-scatter.11.cloned.1.call-done = f32[512,768]{1,0:T(8,128)} async-done(((f32[2048,768]{1,0:T(8,128)}), f32[512,768]{1,0:T(8,128)}) %reduce-scatter.11.cloned.1.call-update) | async-done | bytes 1572880 | tf_op jit(solution)/shard_map/reduce_scatter | solution.py:27
  156.9 27.4 %all-gather.9.cloned.1.call-done = bf16[2048,768]{1,0:T(8,128)(2,1)} async-done(((bf16[512,768]{1,0:T(8,128)(2,1)}), bf16[2048,768]{1,0:T(8,128)(2,1)}) %all-gather.9.cloned.1.call-update) | async-done | bytes 3145744 | tf_op jit(solution)/shard_map/all_gather | solution.py:18
  184.2 18.9 %multiply_convert_fusion.1 = (bf16[2048,768]{1,0:T(8,128)(2,1)}, f32[2048,768]{1,0:T(8,128)}, f32[2048,768]{1,0:T(8,128)}) fusion(f32[768]{0:T(1024)S(1)} %copy-done.32, bf16[2048,768]{1,0:T(8,128)(2,1)} %all-gather.9.cloned.1.call-done, bf16[768,768]{1,0:T(8,128)(2,1)} %all-gather.11.cloned.1.call-done), kind=kOutput, calls=%fused_computation.40 | convolution fusion | flops 2519728128 | bytes 20057088 | tf_op jit(solution)/shard_map/dot_general | solution.py:163
  203.2 12.6 %all-gather.13.cloned.1.call-done = bf16[768,768]{1,0:T(8,128)(2,1)} async-done(((bf16[192,768]{1,0:T(8,128)(2,1)}), bf16[768,768]{1,0:T(8,128)(2,1)}) %all-gather.13.cloned.1.call-update) | async-done | bytes 1179664 | tf_op jit(solution)/shard_map/all_gather | solution.py:143
  215.8 7.5 %fusion.42 = f32[2048,768]{1,0:T(8,128)} fusion(bf16[2048,768]{1,0:T(8,128)(2,1)} %get-tuple-element.256, bf16[768,768]{1,0:T(8,128)(2,1)} %all-gather.13.cloned.1.call-done), kind=kOutput, calls=%fused_computation.115 | convolution fusion | flops 2415919104 | bytes 10616832 | tf_op jit(solution)/shard_map/tc,dc->td/dot_general | solution.py:26
  223.3 58.0 %reduce-scatter.13.cloned.1.call-done = f32[512,768]{1,0:T(8,128)} async-done(((f32[2048,768]{1,0:T(8,128)}), f32[512,768]{1,0:T(8,128)}) %reduce-scatter.13.cloned.1.call-update) | async-done | bytes 1572880 | tf_op jit(solution)/shard_map/reduce_scatter | solution.py:27
  285.0 2.4 convert_reduce_fusion.3
  287.7 28.4 %all-gather.15.cloned.1.call-done = bf16[2048,768]{1,0:T(8,128)(2,1)} async-done(((bf16[512,768]{1,0:T(8,128)(2,1)}), bf16[2048,768]{1,0:T(8,128)(2,1)}) %all-gather.15.cloned.1.call-update) | async-done | bytes 3145744 | tf_op jit(solution)/shard_map/all_gather | solution.py:22
  316.2 11.1 %convert_reduce_fusion = (f32[768]{0:T(1024)}, bf16[2048,768]{1,0:T(8,128)(2,1)S(1)}) fusion(f32[2048,768]{1,0:T(8,128)} %get-tuple-element.257, f32[2048,768]{1,0:T(8,128)} %get-tuple-element.279, f32[768]{0:T(1024)S(1)} %copy-done.32, bf16[2048,768]{1,0:T(8,128)(2,1)} %all-gather.15.cloned.1.call-done, bf16[768,768]{1,0:T(8,128)(2,1)} %all-gather.13.cloned.1.call-done), kind=kOutput, calls=%fused_computation.38 | convolution fusion | flops 2442657024 | bytes 20060160 | tf_op jit(solution)/shard_map/dot_general | solution.py:182
  329.0 4.0 convolution_convert_fusion.1
  333.1 37.8 %reduce-scatter.15.cloned.1.call-done = bf16[512,768]{1,0:T(8,128)(2,1)} async-done(((bf16[2048,768]{1,0:T(8,128)(2,1)}), bf16[512,768]{1,0:T(8,128)(2,1)}) %reduce-scatter.15.cloned.1.call-update) | async-done | bytes 786448 | tf_op jit(solution)/shard_map/reduce_scatter | solution.py:32
  370.9 2.6 multiply_reduce_fusion.1
  373.5 3.3 convert_reduce_fusion.4
  376.9 28.6 %all-gather.17.cloned.1.call-done = bf16[2048,768]{1,0:T(8,128)(2,1)} async-done(((bf16[512,768]{1,0:T(8,128)(2,1)}), bf16[2048,768]{1,0:T(8,128)(2,1)}) %all-gather.17.cloned.1.call-update) | async-done | bytes 3145744 | tf_op jit(solution)/shard_map/all_gather | solution.py:22
  405.5 3.1 convolution_convert_fusion.2
  408.7 54.3 %while.23 = (s32[]{:T(128)}, bf16[2,1024,576]{1,2,0:T(8,128)(2,1)}, bf16[2,1024,192]{1,2,0:T(8,128)(2,1)}, s32[2,1024]{1,0:T(2,128)S(1)}, bf16[2,1024,192]{1,2,0...) while((s32[]{:T(128)}, bf16[2,1024,576]{1,2,0:T(8,128)(2,1)}, ...), condition=%wide.region_17.18_spmd, body=%wide.region_15.17_spmd.sunk | while | flops 2066019328 | bytes 108101744 | solution.py:201
  413.7 3.7 fusion.116
  417.4 7.2 %multiply_reduce_fusion.7 = (f32[3,1024]{1,0:T(4,128)S(1)}, f32[3,1024,1024]{1,2,0:T(8,128)}) fusion(f32[3,1024,1024]{1,2,0:T(8,128)S(1)} %fusion.115, f32[3,1024]{1,0:T(4,128)S(1)} %dynamic-slice_bitcast_fusion.2, pred[1024,1024]{0,1:T(8,128)(4,1)S(1)} %broadcast_compare_fusion.5, bf16[1024,3,64]{0,2,1:T(8,128)(2,1)S(1)} %bitcast.146, ...), kind=kOutput, calls=%fused_computation.16.clone.1 | convolution fusion | flops 418378752 | bytes 27025408 | tf_op jit(solution)/shard_map/while/body/eval_jaxpr/qhd,khd->hqk/dot_general | solution.py:91
  424.6 6.9 %multiply_convert_fusion.3 = bf16[3,1024,1024]{1,2,0:T(8,128)(2,1)S(1)} fusion(f32[3,1024,1024]{1,2,0:T(8,128)} %get-tuple-element.392, f32[3,1024,1024]{1,2,0:T(8,128)S(1)} %fusion.115, f32[3,1024]{1,0:T(4,128)S(1)} %get-tuple-element.393, f32[3,1024]{1,0:T(4,128)S(1)} %dynamic-slice_bitcast_fusion.2, pred[1024,1024]{0,1:T(8,128)(4,1)S(1)} %broadcast_compare_fusion.5), kind=kLoop, calls=%fused_computation.15.clone.1 | loop fusion | flops 18874368 | bytes 32530432 | tf_op jit(solution)/shard_map/while/body/eval_jaxpr/convert_element_type | solution.py:95
  440.7 3.7 fusion.116
  444.5 7.2 %multiply_reduce_fusion.7 = (f32[3,1024]{1,0:T(4,128)S(1)}, f32[3,1024,1024]{1,2,0:T(8,128)}) fusion(f32[3,1024,1024]{1,2,0:T(8,128)S(1)} %fusion.115, f32[3,1024]{1,0:T(4,128)S(1)} %dynamic-slice_bitcast_fusion.2, pred[1024,1024]{0,1:T(8,128)(4,1)S(1)} %broadcast_compare_fusion.5, bf16[1024,3,64]{0,2,1:T(8,128)(2,1)S(1)} %bitcast.146, ...), kind=kOutput, calls=%fused_computation.16.clone.1 | convolution fusion | flops 418378752 | bytes 27025408 | tf_op jit(solution)/shard_map/while/body/eval_jaxpr/qhd,khd->hqk/dot_general | solution.py:91
  451.7 6.9 %multiply_convert_fusion.3 = bf16[3,1024,1024]{1,2,0:T(8,128)(2,1)S(1)} fusion(f32[3,1024,1024]{1,2,0:T(8,128)} %get-tuple-element.392, f32[3,1024,1024]{1,2,0:T(8,128)S(1)} %fusion.115, f32[3,1024]{1,0:T(4,128)S(1)} %get-tuple-element.393, f32[3,1024]{1,0:T(4,128)S(1)} %dynamic-slice_bitcast_fusion.2, pred[1024,1024]{0,1:T(8,128)(4,1)S(1)} %broadcast_compare_fusion.5), kind=kLoop, calls=%fused_computation.15.clone.1 | loop fusion | flops 18874368 | bytes 32530432 | tf_op jit(solution)/shard_map/while/body/eval_jaxpr/convert_element_type | solution.py:95
  463.0 2.1 copy.92
  465.6 2.9 fusion.31
  468.5 2.2 copy.85
  471.1 6.5 convolution_convert_fusion.4
  477.7 6.6 convolution_convert_fusion.3
  484.4 3.7 convolution_convert_fusion.6
  488.2 8.9 %reduce-scatter.25.cloned.1.call-done = bf16[192,576]{1,0:T(8,128)(2,1)} async-done(((bf16[768,576]{1,0:T(8,128)(2,1)}), bf16[192,576]{1,0:T(8,128)(2,1)}) %reduce-scatter.25.cloned.1.call-update) | async-done | bytes 221200
  498.9 28.3 %reduce-scatter.21.cloned.1.call-done = bf16[192,768]{1,0:T(8,128)(2,1)} async-done(((bf16[768,768]{1,0:T(8,128)(2,1)}), bf16[192,768]{1,0:T(8,128)(2,1)}) %reduce-scatter.21.cloned.1.call-update) | async-done | bytes 294928 | tf_op jit(solution)/shard_map/reduce_scatter | solution.py:218
  527.2 30.1 %reduce-scatter.23.cloned.1.call-done = bf16[192,768]{1,0:T(8,128)(2,1)} async-done(((bf16[768,768]{1,0:T(8,128)(2,1)}), bf16[192,768]{1,0:T(8,128)(2,1)}) %reduce-scatter.23.cloned.1.call-update) | async-done | bytes 294928 | tf_op jit(solution)/shard_map/reduce_scatter | solution.py:221
  557.3 22.2 %reduce-scatter.19.cloned.1.call-done = bf16[192,192]{1,0:T(8,128)(2,1)} async-done(((bf16[768,192]{1,0:T(8,128)(2,1)}), bf16[192,192]{1,0:T(8,128)(2,1)}) %reduce-scatter.19.cloned.1.call-update) | async-done | bytes 73744 | tf_op jit(solution)/shard_map/reduce_scatter | solution.py:215
  579.5 5.3 convolution_convert_fusion
  585.6 39.4 %all-reduce = (f32[768]{0:T(1024)}, f32[768]{0:T(1024)}, f32[768]{0:T(1024)}, f32[768]{0:T(1024)}, f32[768]{0:T(1024)}, /*index=5*/f32[768]{0:T(1024)}) all-reduce(f32[768]{0:T(1024)S(1)} %copy-done.24, f32[768]{0:T(1024)S(1)} %copy-done.22, f32[768]{0:T(1024)S(1)} %copy-done.23, ...), channel_id=1, replica_groups=mesh['dp'=2,'row'=4,'col'=4] {'dp','row','col'}, use_global_device_ids=true, to_apply=%region_26.27 | all-reduce | flops 4608 | bytes 36864 | tf_op jit(solution)/shard_map/psum | solution.py:240
  624.9 2.2 convert_reduce_fusion.1
  627.1 22.7 %all-reduce.1 = (f32[576]{0:T(1024)S(1)}, f32[768]{0:T(1024)}) all-reduce(f32[576]{0:T(1024)S(1)} %convert_reduce_fusion.1, f32[768]{0:T(1024)S(1)} %copy-done.27), channel_id=1, replica_groups=mesh['dp'=2,'row'=4,'col'=4] {'dp','row'}, use_global_device_ids=true, to_apply=%region_22.23 | all-reduce | flops 1344 | bytes 10752 | tf_op jit(solution)/shard_map/psum | solution.py:232
  658.1 2.4 convert_add_fusion
  (172 shorter events, 55.7 us)
Async XLA Ops:
  8.0 40.5 %all-gather.7.cloned.1.call-start = ((), (), s32[]{:S(2)}) async-start(), calls=%async_computation.8 | async-start | bytes 3932160 | tf_op jit(solution)/shard_map/all_gather | solution.py:18
  8.8 143.7 %reduce-scatter.11.cloned.1.call-start = ((), (), s32[]{:S(2)}) async-start(), calls=%async_computation.9 | async-start | bytes 7864320 | tf_op jit(solution)/shard_map/reduce_scatter | solution.py:27
  48.5 4.7 copy-start.9
  53.4 2.3 copy-start.15
  58.5 2.8 copy-start
  65.2 5.0 copy-start.10
  70.3 0.9 copy-start.11
  74.1 2.8 copy-start
  80.8 5.0 copy-start.10
  85.9 0.9 copy-start.11
  86.7 6.9 %copy-start.13 = (f32[2,3,1024]{2,1,0:T(4,128)}, f32[2,3,1024]{2,1,0:T(4,128)S(1)}, u32[]{:S(2)}) copy-start(f32[2,3,1024]{2,1,0:T(4,128)S(1)} %get-tuple-element.423) | copy-start | bytes 73732
  88.0 0.9 copy-start.2
  93.6 58.9 %copy-start.8 = (bf16[512,768]{1,0:T(8,128)(2,1)S(1)}, bf16[512,768]{1,0:T(8,128)(2,1)}, u32[]{:S(2)}) copy-start(bf16[512,768]{1,0:T(8,128)(2,1)} %param.22) | copy-start | bytes 2359300
  93.6 58.9 %copy-start.28 = (f32[768]{0:T(1024)S(1)}, f32[768]{0:T(1024)}, u32[]{:S(2)}) copy-start(f32[768]{0:T(1024)} %param.30) | copy-start | bytes 9220
  93.6 60.9 %copy-start.16 = (f32[768]{0:T(1024)S(1)}, f32[768]{0:T(1024)}, u32[]{:S(2)}) copy-start(f32[768]{0:T(1024)} %param.31) | copy-start | bytes 9220
  93.7 60.9 %copy-start.25 = (f32[768]{0:T(1024)S(1)}, f32[768]{0:T(1024)}, u32[]{:S(2)}) copy-start(f32[768]{0:T(1024)} %param.32) | copy-start | bytes 9220
  93.7 63.2 %all-gather.11.cloned.1.call-start = ((), (), s32[]{:S(2)}) async-start(), calls=%async_computation.11 | async-start | bytes 1474560 | tf_op jit(solution)/shard_map/all_gather | solution.py:142
  94.2 90.0 %all-gather.9.cloned.1.call-start = ((), (), s32[]{:S(2)}) async-start(), calls=%async_computation.10 | async-start | bytes 3932160 | tf_op jit(solution)/shard_map/all_gather | solution.py:18
  154.2 30.1 %copy-start.32 = (f32[768]{0:T(1024)S(1)}, f32[768]{0:T(1024)}, u32[]{:S(2)}) copy-start(f32[768]{0:T(1024)} %param.34) | copy-start | bytes 9220
  154.5 216.4 %copy-start.17 = (f32[512]{0:T(512)}, f32[512]{0:T(512)S(1)}, u32[]{:S(2)}) copy-start(f32[512]{0:T(512)S(1)} %add_rsqrt_fusion.1) | copy-start | bytes 6148
  155.7 60.0 %all-gather.13.cloned.1.call-start = ((), (), s32[]{:S(2)}) async-start(), calls=%async_computation.12 | async-start | bytes 1474560 | tf_op jit(solution)/shard_map/all_gather | solution.py:143
  156.3 125.0 %reduce-scatter.13.cloned.1.call-start = ((), (), s32[]{:S(2)}) async-start(), calls=%async_computation.13 | async-start | bytes 7864320 | tf_op jit(solution)/shard_map/reduce_scatter | solution.py:27
  223.2 58.1 %copy-start.29 = (f32[768]{0:T(1024)S(1)}, f32[768]{0:T(1024)}, u32[]{:S(2)}) copy-start(f32[768]{0:T(1024)} %param.36) | copy-start | bytes 9220
  223.3 60.4 %copy-start.5 = (bf16[512,768]{1,0:T(8,128)(2,1)S(1)}, bf16[512,768]{1,0:T(8,128)(2,1)}, u32[]{:S(2)}) copy-start(bf16[512,768]{1,0:T(8,128)(2,1)} %param.39) | copy-start | bytes 2359300
  223.3 60.4 %copy-start.18 = (f32[768]{0:T(1024)S(1)}, f32[768]{0:T(1024)}, u32[]{:S(2)}) copy-start(f32[768]{0:T(1024)} %param.37) | copy-start | bytes 9220
  223.3 92.9 %all-gather.15.cloned.1.call-start = ((), (), s32[]{:S(2)}) async-start(), calls=%async_computation.14 | async-start | bytes 3932160 | tf_op jit(solution)/shard_map/all_gather | solution.py:22
  283.3 1.7 copy-start.6
  283.3 1.7 copy-start.26
  287.5 83.4 %reduce-scatter.15.cloned.1.call-start = ((), (), s32[]{:S(2)}) async-start(), calls=%async_computation.15 | async-start | bytes 3932160 | tf_op jit(solution)/shard_map/reduce_scatter | solution.py:32
  316.2 12.9 %copy-start.31 = (bf16[768,768]{1,0:T(8,128)(2,1)S(1)}, bf16[768,768]{1,0:T(8,128)(2,1)}, u32[]{:S(2)}) copy-start(bf16[768,768]{1,0:T(8,128)(2,1)} %all-gather.11.cloned.1.call-done) | copy-start | bytes 3538948
  327.3 1.7 copy-start.33
  333.1 72.5 %all-gather.17.cloned.1.call-start = ((), (), s32[]{:S(2)}) async-start(), calls=%async_computation.16 | async-start | bytes 3932160 | tf_op jit(solution)/shard_map/all_gather | solution.py:22
  370.9 2.6 copy-start.7
  373.5 32.0 %copy-start.4 = (bf16[768,192]{1,0:T(8,128)(2,1)S(1)}, bf16[768,192]{1,0:T(8,128)(2,1)}, u32[]{:S(2)}) copy-start(bf16[768,192]{1,0:T(8,128)(2,1)} %all_gather.30) | copy-start | bytes 884740
  376.9 31.8 %copy-start.14 = (f32[2,3,1024]{2,1,0:T(4,128)S(1)}, f32[2,3,1024]{2,1,0:T(4,128)}, u32[]{:S(2)}) copy-start(f32[2,3,1024]{2,1,0:T(4,128)} %copy-done.13) | copy-start | bytes 73732
  376.9 120.2 %reduce-scatter.25.cloned.1.call-start = ((), (), s32[]{:S(2)}) async-start(), calls=%async_computation.21 | async-start | bytes 1228800
  463.0 2.6 copy-start.30
  470.8 56.4 %reduce-scatter.21.cloned.1.call-start = ((), (), s32[]{:S(2)}) async-start(), calls=%async_computation.19 | async-start | bytes 1474560 | tf_op jit(solution)/shard_map/reduce_scatter | solution.py:218
  477.6 6.8 %copy-start.3 = (bf16[2,24,8,1024]{3,2,0,1:T(8,128)(2,1)S(1)}, bf16[2,24,8,1024]{3,2,0,1:T(8,128)(2,1)}, u32[]{:S(2)}) copy-start(bf16[2,24,8,1024]{3,2,0,1:T(8,128)(2,1)} %copy-done.2) | copy-start | bytes 2359300
  477.6 79.6 %reduce-scatter.23.cloned.1.call-start = ((), (), s32[]{:S(2)}) async-start(), calls=%async_computation.20 | async-start | bytes 1474560 | tf_op jit(solution)/shard_map/reduce_scatter | solution.py:221
  484.3 95.1 %reduce-scatter.19.cloned.1.call-start = ((), (), s32[]{:S(2)}) async-start(), calls=%async_computation.18 | async-start | bytes 491520 | tf_op jit(solution)/shard_map/reduce_scatter | solution.py:215
  488.1 162.3 %all-reduce.5.cloned.1.call-start = ((), (), s32[]{:S(2)}) async-start(), calls=%async_computation.22 | async-start | bytes 1966080 | tf_op jit(solution)/shard_map/psum | solution.py:226
  579.4 78.6 %reduce-scatter.17.cloned.1.call-start = ((), (), s32[]{:S(2)}) async-start(), calls=%async_computation.17 | async-start | bytes 3932160 | tf_op jit(solution)/shard_map/reduce_scatter | solution.py:32
  584.8 0.7 copy-start.23
  584.8 0.7 copy-start.24
  584.8 42.3 %copy-start.27 = (f32[768]{0:T(1024)S(1)}, f32[768]{0:T(1024)}, u32[]{:S(2)}) copy-start(f32[768]{0:T(1024)} %get-tuple-element.252) | copy-start | bytes 9220
  624.9 33.2 %copy-start.1 = (f32[512,768]{1,0:T(8,128)S(1)}, f32[512,768]{1,0:T(8,128)}, u32[]{:S(2)}) copy-start(f32[512,768]{1,0:T(8,128)} %get-tuple-element.251) | copy-start | bytes 4718596
  650.4 6.9 %copy-start.12 = (bf16[192,768]{1,0:T(8,128)(2,1)S(1)}, bf16[192,768]{1,0:T(8,128)(2,1)}, u32[]{:S(2)}) copy-start(bf16[192,768]{1,0:T(8,128)(2,1)} %get-tuple-element.245) | copy-start | bytes 884740
  (4 other events, 2.8 us)
Sparse Core Ops, SparseCore 0:
  10.4 31.2 all-gather.6
  93.8 58.6 reduce-scatter.10
  287.6 28.4 all-gather.14
  377.0 28.4 all-gather.16
  579.6 37.5 all-reduce.4
  619.6 37.8 reduce-scatter.16
Sparse Core Ops, SparseCore 1:
  95.7 29.9 all-gather.10
  155.8 28.3 all-gather.8
  185.7 30.1 all-gather.12
  223.3 58.0 reduce-scatter.12
  333.2 37.7 reduce-scatter.14
  470.9 26.2 reduce-scatter.24
  499.3 27.8 reduce-scatter.20
  529.4 27.8 reduce-scatter.22
  560.0 19.4 reduce-scatter.18
where the time goes:
time: 677 us; the launch traced here: 669 us
  waiting for transfers between devices  342 us (51%)
  matrix products  127 us (19%)
  blocking collectives  99.8 us (15%)
  other arithmetic  52.5 us (8%)
  local copies, waits for them, and re-layouts  28.5 us (4%)
  between operations  16.6 us (2%)
    reduce_scatter x2, waiting for transfers between devices, leave_branch(): lax.psum_scatter(partial_sum, 'col', scatter_dimension=0, tiled=True) + bias  116 us
    all_gather x2, waiting for transfers between devices, gather_grads(): return lax.all_gather(grads, 'col', axis=0, tiled=True)  57 us
    psum x1, blocking collectives, shards(): lax.psum((grad_output_bias, grad_gain_one, grad_shift_one, grad_outer_bia...  39.4 us
    reduce_scatter x2, waiting for transfers between devices, back_to_tokens(): lax.psum_scatter(partial_sum.astype(jnp.bfloat16), 'col', scatter_dimensi...  37.8 us
    reduce_scatter x1, waiting for transfers between devices, shards(): lax.psum_scatter(grad_outer.astype(jnp.bfloat16), 'row', scatter_dimensio...  30.1 us
    reduce_scatter x1, waiting for transfers between devices, shards(): lax.psum_scatter(grad_inner.astype(jnp.bfloat16), 'row', scatter_dimensio...  28.3 us
    all_gather x2, waiting for transfers between devices, gather_tokens(): return lax.all_gather(acts, 'col', axis=0, tiled=True)  27.4 us
    psum x1, blocking collectives, shards(): lax.psum((grad_joint_bias, grad_inner_bias), ('dp', 'row'))  22.7 us
  transfers between devices with their start and end apart: 15, of which 11 were waited for; matrix products, arithmetic and copies ran while one was open for 9% of the time, Pallas kernels for 0%

commit v1 on v0

v1 whole, which is shorter than its diff:
```python
import functools

import jax
import jax.numpy as jnp
from jax import lax
from jax.experimental import pallas as pl
from jax.experimental.pallas import tpu as pltpu
from jax.sharding import PartitionSpec as P

HEAD_DIM = 64
EPS_NORM = 1e-12
NEG_FILL = -1e30
SCALE = HEAD_DIM ** (-0.5)
MESH = pl.DeviceIdType.MESH
BF16 = jnp.bfloat16
F32 = jnp.float32
TILE = 256
INV_SQRT2 = 0.7071067811865476
INV_SQRT_2PI = 0.3989422804014327


def dot(left, right, left_dim, right_dim):
    dims = (((left_dim,), (right_dim,)), ((), ()))
    return lax.dot_general(left, right, dims, preferred_element_type=F32)


def flip(index, mask):
    result, bit = index, 0
    while (1 << bit) <= mask:
        if (mask >> bit) & 1:
            result = result + (1 - 2 * lax.rem(index // (1 << bit), 2)) * (1 << bit)
        bit += 1
    return result


def rows_at(start, size):
    return pl.ds(pl.multiple_of(start, 16), size)


class Copies:
    def __init__(self, send_sem, recv_sem):
        self.send_sem, self.recv_sem, self.made = send_sem, recv_sem, []

    def new(self, src, dst, device):
        number = len(self.made)
        copy = pltpu.make_async_remote_copy(
            src_ref=src,
            dst_ref=dst,
            send_sem=self.send_sem.at[number],
            recv_sem=self.recv_sem.at[number],
            device_id=device,
            device_id_type=MESH,
        )
        self.made.append(copy)
        return copy

    def finish(self):
        for copy in self.made:
            copy.wait_send()


def layer_kernel(
    sizes,
    own_joint,
    own_inner,
    own_outer,
    hidden,
    upstream,
    seg_col,
    seg_row,
    own_bias,
    vectors,
    layer_out,
    grad_inputs,
    out_joint,
    out_inner,
    out_outer,
    out_shared,
    out_bias,
    w_joint,
    w_inner,
    w_outer,
    x_full,
    query,
    keys,
    values,
    log_sums,
    head_mixed,
    mixed,
    bias_full,
    first_normed,
    first_scale,
    first_rows,
    activated,
    gelu_slope,
    branch_two,
    branch_one,
    grad_heads,
    send_part,
    recv_part,
    q_turned,
    o_turned,
    dk_turned,
    dv_turned,
    g_joint,
    g_inner,
    g_outer,
    xy_recv,
    z_recv,
    f_send,
    f_recv,
    shared_sum,
    bias_sum,
    shared_pair,
    vec_x,
    vec_dp,
    vec_z,
    send_sem,
    recv_sem,
):
    dp_size, row_size = sizes
    grad_second = grad_inputs
    tokens, width = hidden.shape
    length = 2 * tokens
    block = own_joint.shape[0]
    half = block // 2
    heads = w_joint.shape[2] // (4 * HEAD_DIM)
    piece = heads * HEAD_DIM
    tiles, own_tiles = length // TILE, tokens // TILE
    width_tiles = width // TILE
    dp, row, col = (lax.axis_index(name) for name in ("dp", "row", "col"))
    core, mine = lax.rem(col, 2), col // 2
    other = 1 - mine
    side = lax.rem(dp, 2)
    partner = {"dp": dp, "row": row, "col": flip(col, 1)}
    x_peer = {"dp": dp, "row": row, "col": flip(col, 2)}
    y_peer = {"dp": flip(dp, 1), "row": row, "col": col}
    dp_peers = [{"dp": flip(dp, mask), "row": row, "col": col} for mask in range(1, dp_size)]
    z_peers = [{"dp": dp, "row": flip(row, mask), "col": col} for mask in range(1, row_size)]
    z_of = [flip(row, mask) for mask in range(row_size)]
    copies = Copies(send_sem, recv_sem)

    barrier = pltpu.get_barrier_semaphore()
    everyone = [partner, x_peer] + dp_peers + z_peers
    for peer in everyone:
        pl.semaphore_signal(barrier, inc=1, device_id=peer, device_id_type=MESH)
    pl.semaphore_wait(barrier, len(everyone))

    own_start, far_start = core * tokens, (1 - core) * tokens

    def half_rows(z, which):
        return rows_at(z * block + which * half, half)

    def block_rows(z):
        return rows_at(z * block, block)

    class Gather:
        def __init__(self, own, full):
            self.own, self.full = own, full
            source = own.at[rows_at(side * half, half)]
            spot = full.at[mine, half_rows(row, side)]
            self.z = [copies.new(source, spot, peer) for peer in z_peers]
            self.x_own = copies.new(own, full.at[mine, block_rows(row)], x_peer)
            got = [full.at[mine, half_rows(z, side)] for z in z_of[1:]]
            self.x = [copies.new(ref, ref, x_peer) for ref in got]
            self.y = [copies.new(ref, ref, y_peer) for ref in got]
            got = [full.at[other, half_rows(z, side)] for z in z_of[1:]]
            self.xy = [copies.new(ref, ref, y_peer) for ref in got]

        def start(self):
            self.z[0].start()
            self.x_own.start()

        def near(self):
            self.z[0].wait_recv()
            self.y[0].start()
            self.x[0].start()
            for copy in self.z[1:]:
                copy.start()

        def far(self):
            for z, x, y in list(zip(self.z, self.x, self.y))[1:]:
                z.wait_recv()
                y.start()
                x.start()

        def across(self):
            for x, xy in zip(self.x, self.xy):
                x.wait_recv()
                xy.start()

        def done(self):
            self.x_own.wait_recv()
            for copy in self.y + self.xy:
                copy.wait_recv()

    gathers = [
        Gather(own_joint, w_joint),
        Gather(own_inner, w_inner),
        Gather(own_outer, w_outer),
    ]
    gathers[0].start()
    own_rows_all = rows_at(own_start, tokens)
    send_x = copies.new(hidden, x_full.at[own_rows_all], partner)
    send_x.start()
    send_bias = copies.new(own_bias, bias_full.at[mine], x_peer)
    send_bias.start()
    for own, full in ((own_joint, w_joint), (own_inner, w_inner), (own_outer, w_outer)):
        full[mine, block_rows(row), :] = own[...]
    x_full[own_rows_all, :] = hidden[...]
    bias_full[mine] = own_bias[...]
    shared_sum[...] = jnp.zeros_like(shared_sum)
    bias_sum[...] = jnp.zeros_like(bias_sum)

    gathers[0].near()
    gathers[0].far()
    gathers[1].start()
    gathers[0].across()
    gathers[1].near()
    send_x.wait_recv()
    send_bias.wait_recv()
    gathers[0].done()

    def project(tile, carry):
        rows = rows_at(tile * TILE, TILE)
        x = x_full[rows, :]
        for h in range(2):
            out = dot(x, w_joint[h, :, 128:], 1, 0) + bias_full[h, 0:1, 128:]
            at = piece - 128
            for which, target in enumerate((query, keys, values)):
                for i in range(heads):
                    start = at + which * piece + i * HEAD_DIM
                    part = out[:, start : start + HEAD_DIM].astype(BF16)
                    if which == 0:
                        part = part * SCALE
                    target[h * heads + i, rows, :] = part.astype(BF16)
        return carry

    lax.fori_loop(0, tiles, project, 0)
    gathers[1].far()

    lanes = lax.broadcasted_iota(jnp.int32, (TILE, 128), 1)

    def attend(head):
        def body(tile, carry):
            rows = rows_at(tile * TILE, TILE)
            scores = dot(query[head, rows, :], keys[head], 1, 1)
            scores = jnp.where(seg_col[rows, :] == seg_row[...], scores, NEG_FILL)
            peak = jnp.max(scores, axis=1, keepdims=True)
            expos = jnp.exp(scores - peak)
            total = jnp.sum(expos, axis=1, keepdims=True)
            out = dot(expos.astype(BF16), values[head], 1, 0) / total
            head_mixed[head, rows, :] = out.astype(BF16)
            log_sums[rows, :] = jnp.where(lanes == head, peak + jnp.log(total), log_sums[rows, :])
            return carry

        lax.fori_loop(0, tiles, body, 0)

    services = [
        gathers[1].across,
        gathers[2].start,
        gathers[2].near,
        lambda: (gathers[1].done(), gathers[2].far()),
        gathers[2].across,
        lambda: None,
    ]
    for head in range(2 * heads):
        attend(head)
        services[min(head, len(services) - 1)]()

    def join(tile, carry):
        rows = rows_at(tile * TILE, TILE)
        for h in range(2):
            parts = [head_mixed[h * heads + i, rows, :] for i in range(heads)]
            mixed[h, rows, :] = jnp.concatenate(parts, axis=1)
        return carry

    lax.fori_loop(0, tiles, join, 0)

    class Exchange:
        def __init__(self, number, partial_of):
            self.partial_of = partial_of
            self.send = send_part.at[number % 2]
            self.recv = recv_part.at[number]
            self.copies = [
                copies.new(
                    self.send.at[pl.ds(i * TILE, TILE)],
                    self.recv.at[pl.ds(i * TILE, TILE)],
                    partner,
                )
                for i in range(own_tiles)
            ]

        def give(self):
            for i, copy in enumerate(self.copies):
                part = self.partial_of(rows_at(far_start + i * TILE, TILE))
                self.send[pl.ds(i * TILE, TILE), :] = part.astype(BF16)
                copy.start()

        def take(self, i):
            part = self.partial_of(rows_at(own_start + i * TILE, TILE))
            self.copies[i].wait_recv()
            return part + self.recv[pl.ds(i * TILE, TILE), :].astype(F32)

    class Share:
        def __init__(self, full):
            self.full = full
            spots = [full.at[rows_at(own_start + i * TILE, TILE)] for i in range(own_tiles)]
            self.copies = [copies.new(ref, ref, partner) for ref in spots]

        def put(self, i, tile_rows):
            self.full[rows_at(own_start + i * TILE, TILE), :] = tile_rows
            self.copies[i].start()

        def wait(self):
            for copy in self.copies:
                copy.wait_recv()

    def mean(v):
        return jnp.sum(v, axis=1, keepdims=True) * (1.0 / width)

    def normalize(v):
        centered = v - mean(v)
        inv_scale = lax.rsqrt(mean(centered * centered) + EPS_NORM)
        return centered * inv_scale, inv_scale

    def norm_backward(grads, normed, inv_scale, gain):
        scaled = grads * gain
        return inv_scale * (scaled - mean(scaled) - normed * mean(scaled * normed))

    def add_shared(index, v):
        shared_sum[index : index + 1, :] += jnp.sum(v, axis=0, keepdims=True)

    def mixed_partial(rows):
        return dot(mixed[0, rows, :], w_joint[0, :, :piece], 1, 1) + dot(
            mixed[1, rows, :], w_joint[1, :, :piece], 1, 1
        )

    leave_one = Exchange(0, mixed_partial)
    leave_one.give()
    share_first = Share(first_rows)
    for i in range(own_tiles):
        rows = pl.ds(i * TILE, TILE)
        branch = leave_one.take(i) + vectors[0:1, :]
        normed, inv_scale = normalize(hidden[rows, :].astype(F32) + branch)
        first_normed[rows, :] = normed
        first_scale[rows, :] = inv_scale
        out = normed * vectors[1:2, :] + vectors[2:3, :]
        share_first.put(i, out.astype(BF16))

    def inner(tile, start):
        rows = rows_at(start + tile * TILE, TILE)
        x = first_rows[rows, :]
        for h in range(2):
            pre = dot(x, w_inner[h], 1, 0) + bias_full[h, 1:2, :]
            below = 0.5 + 0.5 * lax.erf(pre * INV_SQRT2)
            density = INV_SQRT_2PI * jnp.exp(-0.5 * pre * pre)
            activated[h, rows, :] = (pre * below).astype(BF16)
            gelu_slope[h, rows, :] = (below + pre * density).astype(BF16)
        return start

    lax.fori_loop(0, own_tiles, inner, own_start)
    share_first.wait()
    lax.fori_loop(0, own_tiles, inner, far_start)
    gathers[2].done()

    def outer_partial(rows):
        return dot(activated[0, rows, :], w_outer[0], 1, 1) + dot(
            activated[1, rows, :], w_outer[1], 1, 1
        )

    leave_two = Exchange(1, outer_partial)
    leave_two.give()
    share_two = Share(branch_two)
    for i in range(own_tiles):
        rows = pl.ds(i * TILE, TILE)
        branch = leave_two.take(i) + vectors[3:4, :]
        normed, inv_scale = normalize(
            first_normed[rows, :] * vectors[1:2, :] + vectors[2:3, :] + branch
        )
        layer_out[rows, :] = (normed * vectors[4:5, :] + vectors[5:6, :]).astype(BF16)
        grads = upstream[rows, :].astype(F32)
        back = norm_backward(grads, normed, inv_scale, vectors[4:5, :])
        grad_second[rows, :] = back
        rounded = back.astype(BF16)
        share_two.put(i, rounded)
        add_shared(3, rounded.astype(F32))
        add_shared(4, grads * normed)
        add_shared(5, grads)
    share_two.wait()

    class Reduce:
        def __init__(self, number, grads, out, x_first):
            self.grads, self.out, self.x_first = grads, out, x_first
            self.pool = pool = xy_recv.at[number]
            self.late = late = [rows_at(width + z * half, half) for z in z_of]
            self.zr, self.fs, self.fr = z_recv.at[number], f_send.at[number], f_recv.at[number]
            away = 1 - side
            if x_first:
                self.first = [
                    copies.new(grads.at[other, block_rows(z)], pool.at[block_rows(z)], x_peer)
                    for z in z_of
                ]
                self.second = [
                    copies.new(
                        grads.at[mine, half_rows(z, away)],
                        pool.at[late[j]],
                        y_peer,
                    )
                    for j, z in enumerate(z_of)
                ]
            else:
                self.first = [
                    copies.new(
                        grads.at[h, half_rows(z, away)], pool.at[self.early(h, z)], y_peer
                    )
                    for h in (other, mine)
                    for z in z_of
                ]
                self.second = [
                    copies.new(
                        grads.at[other, half_rows(z, side)],
                        pool.at[late[j]],
                        x_peer,
                    )
                    for j, z in enumerate(z_of)
                ]
            self.third = [
                copies.new(
                    grads.at[mine, half_rows(z, side)],
                    self.zr.at[mask],
                    peer,
                )
                for mask, (z, peer) in enumerate(zip(z_of[1:], z_peers))
            ]
            self.fourth = [copies.new(self.fs, self.fr.at[dp], peer) for peer in dp_peers]
            self.order = list(range(1, row_size)) + [0]

        def early(self, h, z):
            return rows_at(h * (width // 2) + z * half, half)

        def start(self):
            for j in self.order:
                self.first[j].start()

        def start_rest(self):
            for j in self.order:
                self.first[row_size + j].start()

        def add(self, rows, h, recv):
            total = self.grads[h, rows, :].astype(F32) + recv.astype(F32)
            self.grads[h, rows, :] = total.astype(BF16)

        def go_second(self):
            for j in self.order:
                z = z_of[j]
                self.first[j].wait_recv()
                if self.x_first:
                    self.add(block_rows(z), mine, self.pool[block_rows(z), :])
                else:
                    self.add(half_rows(z, side), other, self.pool[self.early(other, z), :])
                self.second[j].start()

        def go_third(self):
            for j in self.order:
                z = z_of[j]
                rows = half_rows(z, side)
                if not self.x_first:
                    self.first[row_size + j].wait_recv()
                self.second[j].wait_recv()
                if self.x_first:
                    self.add(rows, mine, self.pool[self.late[j], :])
                else:
                    total = (
                        self.grads[mine, rows, :].astype(F32)
                        + self.pool[self.early(mine, z), :].astype(F32)
                        + self.pool[self.late[j], :].astype(F32)
                    )
                    self.grads[mine, rows, :] = total.astype(BF16)
                if j:
                    self.third[j - 1].start()

        def go_fourth(self):
            total = self.grads[mine, half_rows(row, side), :].astype(F32)
            for mask, copy in enumerate(self.third):
                copy.wait_recv()
                total = total + self.zr[mask].astype(F32)
            self.fs[...] = total.astype(BF16)
            for copy in self.fourth:
                copy.start()

        def done(self):
            for copy in self.fourth:
                copy.wait_recv()
            self.fr[dp] = self.fs[...]
            for which in range(2):
                total = self.fr[which].astype(F32)
                for index in range(which + 2, dp_size, 2):
                    total = total + self.fr[index].astype(F32)
                self.out[pl.ds(which * half, half), :] = total

    reduce_outer = Reduce(0, g_outer, out_outer, True)
    reduce_inner = Reduce(1, g_inner, out_inner, False)
    reduce_joint = Reduce(2, g_joint, out_joint, True)

    def weight_grad(target, rows_of, cols_of, h):
        def body(tile, carry):
            at = pl.ds(pl.multiple_of(tile * TILE, TILE), TILE)
            target[h, at, :] = dot(rows_of[:, at], cols_of[h], 0, 0).astype(BF16)
            return carry

        lax.fori_loop(0, width_tiles, body, 0)

    weight_grad(g_outer, branch_two, activated, other)
    reduce_outer.start()

    def back_inner(tile, carry):
        rows = rows_at(tile * TILE, TILE)
        g = branch_two[rows, :]
        for h in range(2):
            back = dot(g, w_outer[h], 1, 0) * gelu_slope[h, rows, :].astype(F32)
            rounded = back.astype(BF16)
            gelu_slope[h, rows, :] = rounded
            bias_sum[h, 1:2, :] += jnp.sum(rounded.astype(F32), axis=0, keepdims=True)
        return carry

    lax.fori_loop(0, tiles, back_inner, 0)

    def inner_back_partial(rows):
        return dot(gelu_slope[0, rows, :], w_inner[0], 1, 1) + dot(
            gelu_slope[1, rows, :], w_inner[1], 1, 1
        )

    back_one = Exchange(2, inner_back_partial)
    for copy in leave_one.copies:
        copy.wait_send()
    back_one.give()
    weight_grad(g_outer, branch_two, activated, mine)
    share_one = Share(branch_one)
    for i in range(own_tiles):
        rows = pl.ds(i * TILE, TILE)
        grads = back_one.take(i) + grad_second[rows, :]
        normed = first_normed[rows, :]
        back = norm_backward(grads, normed, first_scale[rows, :], vectors[1:2, :])
        grad_second[rows, :] = back
        rounded = back.astype(BF16)
        share_one.put(i, rounded)
        add_shared(0, rounded.astype(F32))
        add_shared(1, grads * normed)
        add_shared(2, grads)
    send_shared = copies.new(shared_sum, shared_pair, partner)
    send_shared.start()
    weight_grad(g_inner, first_rows, gelu_slope, other)
    reduce_inner.start()
    weight_grad(g_inner, first_rows, gelu_slope, mine)
    reduce_inner.start_rest()
    share_one.wait()

    def back_mixed(tile, carry):
        rows = rows_at(tile * TILE, TILE)
        g = branch_one[rows, :]
        for h in range(2):
            out = dot(g, w_joint[h, :, :piece], 1, 0)
            for i in range(heads):
                part = out[:, i * HEAD_DIM : (i + 1) * HEAD_DIM]
                grad_heads[h * heads + i, rows, :] = part.astype(BF16)
        return carry

    lax.fori_loop(0, tiles, back_mixed, 0)
    reduce_outer.go_second()

    def attend_back(head, carry):
        q_turned[...] = query[head].T
        o_turned[...] = grad_heads[head].T
        dk_turned[...] = jnp.zeros_like(dk_turned)
        dv_turned[...] = jnp.zeros_like(dv_turned)

        def body(tile, carry):
            rows = rows_at(tile * TILE, TILE)
            q, g = query[head, rows, :], grad_heads[head, rows, :]
            scores = dot(q, keys[head], 1, 1)
            scores = jnp.where(seg_col[rows, :] == seg_row[...], scores, NEG_FILL)
            log_sum = jnp.sum(
                jnp.where(lanes == head, log_sums[rows, :], 0.0), axis=1, keepdims=True
            )
            probs = jnp.exp(scores - log_sum)
            grad_probs = dot(g, values[head], 1, 1)
            inner_sum = jnp.sum(
                g.astype(F32) * head_mixed[head, rows, :].astype(F32), axis=1, keepdims=True
            )
            grad_scores = (probs * (grad_probs - inner_sum)).astype(BF16)
            dv_turned[...] += dot(o_turned[:, rows], probs.astype(BF16), 1, 0)
            dk_turned[...] += dot(q_turned[:, rows], grad_scores, 1, 0)
            query[head, rows, :] = (dot(grad_scores, keys[head], 1, 0) * SCALE).astype(BF16)
            return carry

        lax.fori_loop(0, tiles, body, 0)
        keys[head] = dk_turned[...].T.astype(BF16)
        values[head] = dv_turned[...].T.astype(BF16)
        return carry

    grad_rows = activated

    def gather_heads(h):
        def body(tile, carry):
            rows = rows_at(tile * TILE, TILE)
            parts = [jnp.zeros((TILE, piece), BF16)]
            for source in (query, keys, values):
                for i in range(heads):
                    parts.append(source[h * heads + i, rows, :])
            joined = jnp.concatenate(parts, axis=1)
            grad_rows[h, rows, :] = joined
            bias_sum[h, 0:1, :] += jnp.sum(joined.astype(F32), axis=0, keepdims=True)
            return carry

        lax.fori_loop(0, tiles, body, 0)

        def joint_grad(tile, carry):
            at = pl.ds(pl.multiple_of(tile * TILE, TILE), TILE)
            g_joint[h, at, :] = dot(x_full[:, at], grad_rows[h], 0, 0).astype(BF16)
            g_joint[h, at, :piece] = dot(branch_one[:, at], mixed[h], 0, 0).astype(BF16)
            return carry

        lax.fori_loop(0, width_tiles, joint_grad, 0)

    attend_back(other * heads, 0)
    reduce_outer.go_third()
    attend_back(other * heads + 1, 0)
    reduce_inner.go_second()
    lax.fori_loop(other * heads + 2, other * heads + heads, attend_back, 0)
    gather_heads(other)
    reduce_joint.start()
    reduce_outer.go_fourth()
    attend_back(mine * heads, 0)
    reduce_inner.go_third()
    attend_back(mine * heads + 1, 0)
    reduce_inner.go_fourth()
    reduce_outer.done()
    lax.fori_loop(mine * heads + 2, mine * heads + heads, attend_back, 0)
    gather_heads(mine)

    send_shared.wait_recv()
    vec_x_send, vec_x_recv = vec_x.at[0], vec_x.at[1]
    vec_x[0, :8, :] = shared_sum[...] + shared_pair[...]
    vec_x[0, 8:, :] = bias_sum[other]
    send_vec_x = copies.new(vec_x_send, vec_x_recv, x_peer)
    send_vec_x.start()

    reduce_joint.go_second()

    def input_partial(rows):
        return dot(grad_rows[0, rows, :], w_joint[0], 1, 1) + dot(
            grad_rows[1, rows, :], w_joint[1], 1, 1
        )

    back_two = Exchange(3, input_partial)
    for copy in leave_two.copies:
        copy.wait_send()
    back_two.give()

    send_vec_x.wait_recv()
    vec_dp[dp, :8, :] = vec_x[0, :8, :] + vec_x[1, :8, :]
    vec_dp[dp, 8:, :] = bias_sum[mine] + vec_x[1, 8:, :]
    send_vec_dp = [copies.new(vec_dp.at[dp], vec_dp.at[dp], peer) for peer in dp_peers]
    for copy in send_vec_dp:
        copy.start()

    reduce_inner.done()
    reduce_joint.go_third()
    for i in range(own_tiles):
        rows = pl.ds(i * TILE, TILE)
        grad_inputs[rows, :] = back_two.take(i) + grad_second[rows, :]

    for copy in send_vec_dp:
        copy.wait_recv()
    total = vec_dp[0]
    for index in range(1, dp_size):
        total = total + vec_dp[index]
    vec_z[row] = total
    send_vec_z = [copies.new(vec_z.at[row], vec_z.at[row], peer) for peer in z_peers]
    for copy in send_vec_z:
        copy.start()

    reduce_joint.go_fourth()
    for copy in send_vec_z:
        copy.wait_recv()
    total = vec_z[0]
    for index in range(1, row_size):
        total = total + vec_z[index]
    out_shared[...] = total[:8]
    out_bias[...] = total[8:]
    reduce_joint.done()

    waited = set(map(id, leave_one.copies + leave_two.copies))
    for copy in copies.made:
        if id(copy) not in waited:
            copy.wait_send()


def shards(
    mesh_shape,
    hidden,
    segments,
    query_weight,
    key_weight,
    value_weight,
    query_bias,
    value_bias,
    output_weight,
    output_bias,
    first_gain,
    first_shift,
    inner_weight,
    inner_bias,
    outer_weight,
    outer_bias,
    second_gain,
    second_shift,
    upstream,
):
    dp_size, row_size, col_size = mesh_shape
    tokens, width = hidden.shape
    length = segments.shape[1]
    block, piece = query_weight.shape
    hidden_units = inner_weight.shape[1]
    heads = piece // HEAD_DIM
    assert col_size == 4 and length == 2 * tokens and 4 * piece == width == hidden_units
    joint = jnp.concatenate([output_weight, query_weight, key_weight, value_weight], axis=1)
    none = jnp.zeros((piece,), F32)
    joint_bias = jnp.concatenate([none, query_bias, none, value_bias])
    own_bias = jnp.zeros((8, width), F32).at[0].set(joint_bias).at[1].set(inner_bias)
    vectors = jnp.stack(
        [output_bias, first_gain, first_shift, outer_bias, second_gain, second_shift]
        + [jnp.zeros_like(output_bias)] * 2
    )
    segment = lax.dynamic_index_in_dim(segments, lax.axis_index("col") // 2, 0, keepdims=True)
    seg_col = segment.reshape(length, 1)
    half = block // 2
    vmem = pl.BlockSpec(memory_space=pltpu.VMEM)

    def shape(dims, dtype):
        return jax.ShapeDtypeStruct(dims, dtype)

    per_head = pltpu.VMEM((2 * heads, length, HEAD_DIM), BF16)
    weights = pltpu.VMEM((2, width, width), BF16)
    scratch = [
        weights,
        weights,
        weights,
        pltpu.VMEM((length, width), BF16),
        per_head,
        per_head,
        per_head,
        pltpu.VMEM((length, 128), F32),
        per_head,
        pltpu.VMEM((2, length, piece), BF16),
        pltpu.VMEM((2, 8, width), F32),
        pltpu.VMEM((tokens, width), F32),
        pltpu.VMEM((tokens, 1), F32),
        pltpu.VMEM((length, width), BF16),
        pltpu.VMEM((2, length, width), BF16),
        pltpu.VMEM((2, length, width), BF16),
        pltpu.VMEM((length, width), BF16),
        pltpu.VMEM((length, width), BF16),
        per_head,
        pltpu.VMEM((2, tokens, width), BF16),
        pltpu.VMEM((4, tokens, width), BF16),
        pltpu.VMEM((HEAD_DIM, length), BF16),
        pltpu.VMEM((HEAD_DIM, length), BF16),
        pltpu.VMEM((HEAD_DIM, length), F32),
        pltpu.VMEM((HEAD_DIM, length), F32),
        weights,
        weights,
        weights,
        pltpu.VMEM((3, 3 * width // 2, width), BF16),
        pltpu.VMEM((3, row_size - 1, half, width), BF16),
        pltpu.VMEM((3, half, width), BF16),
        pltpu.VMEM((3, dp_size, half, width), BF16),
        pltpu.VMEM((8, width), F32),
        pltpu.VMEM((2, 8, width), F32),
        pltpu.VMEM((8, width), F32),
        pltpu.VMEM((2, 16, width), F32),
        pltpu.VMEM((dp_size, 16, width), F32),
        pltpu.VMEM((row_size, 16, width), F32),
        pltpu.SemaphoreType.DMA((256,)),
        pltpu.SemaphoreType.DMA((256,)),
    ]
    (
        layer_out,
        grad_inputs,
        grad_joint,
        grad_inner,
        grad_outer,
        shared,
        biases,
    ) = pl.pallas_call(
        functools.partial(layer_kernel, (dp_size, row_size)),
        out_shape=[
            shape((tokens, width), BF16),
            shape((tokens, width), F32),
            shape((block, width), F32),
            shape((block, width), F32),
            shape((block, width), F32),
            shape((8, width), F32),
            shape((8, width), F32),
        ],
        in_specs=[vmem] * 9,
        out_specs=[vmem] * 7,
        scratch_shapes=scratch,
        compiler_params=pltpu.CompilerParams(
            collective_id=0, has_side_effects=True, vmem_limit_bytes=67043328
        ),
        name="layer",
    )(
        joint,
        inner_weight,
        outer_weight,
        hidden,
        upstream,
        seg_col,
        segment,
        own_bias,
        vectors,
    )
    return (
        layer_out,
        grad_inputs,
        grad_joint[:, piece : 2 * piece],
        grad_joint[:, 2 * piece : 3 * piece],
        grad_joint[:, 3 * piece :],
        biases[0, piece : 2 * piece],
        biases[0, 3 * piece :],
        grad_joint[:, :piece],
        shared[0],
        shared[1],
        shared[2],
        grad_inner,
        biases[1],
        grad_outer,
        shared[3],
        shared[4],
        shared[5],
    )


def solution(mesh):
    tokens_spec = P(("dp", "row", "col"), None)
    weight_spec = P("row", "col")
    in_specs = (
        tokens_spec,
        P(("dp", "row"), None),
        weight_spec,
        weight_spec,
        weight_spec,
        P("col"),
        P("col"),
        weight_spec,
        P(),
        P(),
        P(),
        weight_spec,
        P("col"),
        weight_spec,
        P(),
        P(),
        P(),
        tokens_spec,
    )
    out_specs = (
        tokens_spec,
        tokens_spec,
        weight_spec,
        weight_spec,
        weight_spec,
        P("col"),
        P("col"),
        weight_spec,
        P(),
        P(),
        P(),
        weight_spec,
        P("col"),
        weight_spec,
        P(),
        P(),
        P(),
    )
    mesh_shape = (mesh.shape["dp"], mesh.shape["row"], mesh.shape["col"])
    return jax.shard_map(
        functools.partial(shards, mesh_shape),
        mesh=mesh,
        in_specs=in_specs,
        out_specs=out_specs,
        check_vma=False,
    )
```

time: 677 us -> 240 us (0.35); the launches traced: 669 us -> 240 us
  waiting for transfers between devices: 342 us -> 0 us
  Pallas kernels: 0 us -> 217 us
  matrix products: 127 us -> 0 us
  blocking collectives: 99.8 us -> 0 us
  other arithmetic: 52.5 us -> 2.66 us
  between operations: 16.6 us -> 0.7 us
  local copies, waits for them, and re-layouts: 28.5 us -> 19.6 us
    reduce_scatter x7 -> x0, waiting for transfers between devices: 234 us -> none  [the longest x2 116 us: leave_branch(): lax.psum_scatter(partial_sum, 'col', scatter_dimension=0, tiled=True) + bias]
    pallas_call x0 -> x1, Pallas kernels: none -> 217 us  [shards(): pl.pallas_call(functools.partial(layer_kernel, (dp_size, row_size)), out_...]
    dot_general x26 -> x0, matrix products: 127 us -> none  [the longest x1 18.9 us: shards(): jnp.dot(first_rows, inner_full, preferred_element_type=jnp.float32)]
    all_gather x6 -> x0, waiting for transfers between devices: 97 us -> none  [the longest x2 57 us: gather_grads(): return lax.all_gather(grads, 'col', axis=0, tiled=True)]
    psum x2 -> x0, blocking collectives: 62 us -> none  [the longest x1 39.4 us: shards(): lax.psum((grad_output_bias, grad_gain_one, grad_shift_one, grad_outer_bia...]
    all_gather x2 -> x0, blocking collectives: 37.8 us -> none  [the longest x1 19.6 us: shards(): lax.all_gather(joint_shard, 'row', axis=0, tiled=True)]
    reduce_sum x11 -> x0, other arithmetic: 23.9 us -> none  [the longest x2 7.73 us: attend_forward(): totals = jnp.sum(expos, axis=2, keepdims=True)]
    convert_element_type x6 -> x0, other arithmetic: 19.4 us -> none  [the longest x2 13.9 us: attend_backward(): grad_scores = (probs * (grad_probs - inner_sum)).astype(jnp.bfloat16)]
  transfers between devices with their start and end apart: 15 -> 0, of which waited for: 11 -> 0; matrix products, arithmetic and copies ran while one was open for 9% -> 0% of each run, Pallas kernels for 0% -> 0%
where the time goes in v1:
time: 240 us
  Pallas kernels  217 us (90%)
  local copies, waits for them, and re-layouts  19.6 us (8%)
  other arithmetic  2.66 us (1%)
    pallas_call x1, Pallas kernels, shards(): pl.pallas_call(functools.partial(layer_kernel, (dp_size, row_size)), out_...  217 us

profile of v1, /device:TPU:0, one launch (start us, length us, event | category | flops | bytes accessed | tf_op | source)
XLA Modules:
  0.0 239.8 jit_solution(5129246721999699594)
XLA Ops:
  0.7 1.9 pad_maximum_fusion.own_joint
  2.5 0.7 fusion.2
  3.2 1.0 copy.35.seg_col
  4.3 1.3 constant_dynamic-slice_fusion.seg_row
  5.6 0.8 pad_maximum_fusion.1
  6.3 0.6 scatter.6
  7.0 0.7 reshape.91
  7.7 1.4 scatter.9.own_bias
  9.0 0.7 stack.24
  9.7 0.7 stack.25
  10.4 0.7 stack.26
  11.1 0.7 stack.27
  11.8 0.7 stack.28
  12.5 0.7 stack.29
  13.2 0.6 stack.31.vectors
  13.8 216.8 %layer.1 = (bf16[512,768]{1,0:T(8,128)(2,1)}, f32[512,768]{1,0:T(8,128)}, f32[192,768]{1,0:T(8,128)}, f32[192,768]{1,0:T(8,128)}, f32[192,768]{1,0:T(8,128)}, /*index=5*/f32[8,768]{1,0:T(8,128)}, f32[8,768]{1,0:T(8,128)}) custom-call(bf16[192,768]{1,0:T(8,128)(2,1)} %pad_maximum_fusion.own_joint, bf16[192,768]{1,0:T(8,128)(2,1)} %own_inner.1, ...), custom_call_target="tpu_custom_call" | custom-call | tf_op jit(solution)/shard_map/layer/pallas_call | solution.py:796
  230.6 0.0 copy-start.4
  230.6 0.0 copy-start.1
  230.6 0.0 copy-start
  230.6 2.4 fusion
  233.0 1.4 fusion.1
  234.4 0.0 copy-done.4
  234.4 1.4 slice_reduce_fusion
  235.8 0.0 copy-done.1
  235.8 0.9 copy.41
  236.7 0.0 copy-done
  236.7 0.0 copy-start.3
  236.7 0.0 copy-start.2
  236.7 1.1 copy.42
  237.8 0.3 copy-done.3
  238.1 0.8 copy.43
  238.9 0.0 copy-done.2
  239.0 0.8 copy.44
  (3 shorter events, 0.0 us)
Async XLA Ops:
  230.6 3.8 %copy-start.4 = (f32[8,768]{1,0:T(8,128)S(1)}, f32[8,768]{1,0:T(8,128)}, u32[]{:S(2)}) copy-start(f32[8,768]{1,0:T(8,128)} %get-tuple-element.52) | copy-start | bytes 73732
  230.6 5.2 %copy-start.1 = (bf16[512,768]{1,0:T(8,128)(2,1)S(1)}, bf16[512,768]{1,0:T(8,128)(2,1)}, u32[]{:S(2)}) copy-start(bf16[512,768]{1,0:T(8,128)(2,1)} %get-tuple-element.85) | copy-start | bytes 2359300
  230.6 6.1 %copy-start = (f32[512,768]{1,0:T(8,128)S(1)}, f32[512,768]{1,0:T(8,128)}, u32[]{:S(2)}) copy-start(f32[512,768]{1,0:T(8,128)} %get-tuple-element.86) | copy-start | bytes 4718596
  236.7 1.4 copy-start.3
  236.7 2.3 copy-start.2

commit v2 on v1

--- a/solution.py
+++ b/solution.py
@@ -33,8 +33,29 @@
     return result
 
 
+def row_of(ref):
+    return ref[...].reshape(1, ref.shape[0])
+
+
 def rows_at(start, size):
     return pl.ds(pl.multiple_of(start, 16), size)
+
+
+class Copy:
+    def __init__(self, descriptor):
+        self.descriptor, self.started, self.sent = descriptor, False, False
+
+    def start(self):
+        self.descriptor.start()
+        self.started = True
+
+    def wait_recv(self):
+        self.descriptor.wait_recv()
+
+    def wait_send(self):
+        if self.started and not self.sent:
+            self.descriptor.wait_send()
+            self.sent = True
 
 
 class Copies:
@@ -43,13 +64,15 @@
 
     def new(self, src, dst, device):
         number = len(self.made)
-        copy = pltpu.make_async_remote_copy(
-            src_ref=src,
-            dst_ref=dst,
-            send_sem=self.send_sem.at[number],
-            recv_sem=self.recv_sem.at[number],
-            device_id=device,
-            device_id_type=MESH,
+        copy = Copy(
+            pltpu.make_async_remote_copy(
+                src_ref=src,
+                dst_ref=dst,
+                send_sem=self.send_sem.at[number],
+                recv_sem=self.recv_sem.at[number],
+                device_id=device,
+                device_id_type=MESH,
+            )
         )
         self.made.append(copy)
         return copy
@@ -61,15 +84,24 @@
 
 def layer_kernel(
     sizes,
-    own_joint,
+    output_weight,
+    query_weight,
+    key_weight,
+    value_weight,
     own_inner,
     own_outer,
     hidden,
     upstream,
-    seg_col,
-    seg_row,
-    own_bias,
-    vectors,
+    segments,
+    query_bias,
+    value_bias,
+    inner_bias,
+    output_bias,
+    first_gain,
+    first_shift,
+    outer_bias,
+    second_gain,
+    second_shift,
     layer_out,
     grad_inputs,
     out_joint,
@@ -77,6 +109,10 @@
     out_outer,
     out_shared,
     out_bias,
+    own_joint,
+    seg_col,
+    seg_row,
+    own_bias,
     w_joint,
     w_inner,
     w_outer,
@@ -140,6 +176,12 @@
     z_of = [flip(row, mask) for mask in range(row_size)]
     copies = Copies(send_sem, recv_sem)
 
+    parts = [output_weight[...], query_weight[...], key_weight[...], value_weight[...]]
+    own_joint[...] = jnp.concatenate(parts, axis=1)
+    none = jnp.zeros((1, piece), F32)
+    joint_bias = jnp.concatenate([none, row_of(query_bias), none, row_of(value_bias)], axis=1)
+    rest = jnp.zeros((6, width), F32)
+    own_bias[...] = jnp.concatenate([joint_bias, row_of(inner_bias), rest], axis=0)
     barrier = pltpu.get_barrier_semaphore()
     everyone = [partner, x_peer] + dp_peers + z_peers
     for peer in everyone:
@@ -209,6 +251,8 @@
         full[mine, block_rows(row), :] = own[...]
     x_full[own_rows_all, :] = hidden[...]
     bias_full[mine] = own_bias[...]
+    seg_row[...] = jnp.where(mine == 0, segments[0:1, :], segments[1:2, :]).astype(F32)
+    seg_col[...] = jnp.broadcast_to(seg_row[...], (128, length)).T
     shared_sum[...] = jnp.zeros_like(shared_sum)
     bias_sum[...] = jnp.zeros_like(bias_sum)
 
@@ -245,7 +289,7 @@
         def body(tile, carry):
             rows = rows_at(tile * TILE, TILE)
             scores = dot(query[head, rows, :], keys[head], 1, 1)
-            scores = jnp.where(seg_col[rows, :] == seg_row[...], scores, NEG_FILL)
+            scores = jnp.where(seg_col[rows, 0:1] == seg_row[...], scores, NEG_FILL)
             peak = jnp.max(scores, axis=1, keepdims=True)
             expos = jnp.exp(scores - peak)
             total = jnp.sum(expos, axis=1, keepdims=True)
@@ -341,11 +385,11 @@
     share_first = Share(first_rows)
     for i in range(own_tiles):
         rows = pl.ds(i * TILE, TILE)
-        branch = leave_one.take(i) + vectors[0:1, :]
+        branch = leave_one.take(i) + row_of(output_bias)
         normed, inv_scale = normalize(hidden[rows, :].astype(F32) + branch)
         first_normed[rows, :] = normed
         first_scale[rows, :] = inv_scale
-        out = normed * vectors[1:2, :] + vectors[2:3, :]
+        out = normed * row_of(first_gain) + row_of(first_shift)
         share_first.put(i, out.astype(BF16))
 
     def inner(tile, start):
@@ -374,13 +418,13 @@
     share_two = Share(branch_two)
     for i in range(own_tiles):
         rows = pl.ds(i * TILE, TILE)
-        branch = leave_two.take(i) + vectors[3:4, :]
+        branch = leave_two.take(i) + row_of(outer_bias)
         normed, inv_scale = normalize(
-            first_normed[rows, :] * vectors[1:2, :] + vectors[2:3, :] + branch
+            first_normed[rows, :] * row_of(first_gain) + row_of(first_shift) + branch
         )
-        layer_out[rows, :] = (normed * vectors[4:5, :] + vectors[5:6, :]).astype(BF16)
+        layer_out[rows, :] = (normed * row_of(second_gain) + row_of(second_shift)).astype(BF16)
         grads = upstream[rows, :].astype(F32)
-        back = norm_backward(grads, normed, inv_scale, vectors[4:5, :])
+        back = norm_backward(grads, normed, inv_scale, row_of(second_gain))
         grad_second[rows, :] = back
         rounded = back.astype(BF16)
         share_two.put(i, rounded)
@@ -541,7 +585,7 @@
         rows = pl.ds(i * TILE, TILE)
         grads = back_one.take(i) + grad_second[rows, :]
         normed = first_normed[rows, :]
-        back = norm_backward(grads, normed, first_scale[rows, :], vectors[1:2, :])
+        back = norm_backward(grads, normed, first_scale[rows, :], row_of(first_gain))
         grad_second[rows, :] = back
         rounded = back.astype(BF16)
         share_one.put(i, rounded)
@@ -579,7 +623,7 @@
             rows = rows_at(tile * TILE, TILE)
             q, g = query[head, rows, :], grad_heads[head, rows, :]
             scores = dot(q, keys[head], 1, 1)
-            scores = jnp.where(seg_col[rows, :] == seg_row[...], scores, NEG_FILL)
+            scores = jnp.where(seg_col[rows, 0:1] == seg_row[...], scores, NEG_FILL)
             log_sum = jnp.sum(
                 jnp.where(lanes == head, log_sums[rows, :], 0.0), axis=1, keepdims=True
             )
@@ -691,10 +735,46 @@
     out_bias[...] = total[8:]
     reduce_joint.done()
 
-    waited = set(map(id, leave_one.copies + leave_two.copies))
-    for copy in copies.made:
-        if id(copy) not in waited:
-            copy.wait_send()
+    copies.finish()
+
+
+def unpack_kernel(
+    layer_in,
+    inputs_in,
+    joint_in,
+    inner_in,
+    outer_in,
+    shared_in,
+    bias_in,
+    layer_out,
+    inputs_out,
+    query_out,
+    key_out,
+    value_out,
+    output_out,
+    inner_out,
+    outer_out,
+    query_bias_out,
+    value_bias_out,
+    *vectors_out,
+):
+    piece, width = query_out.shape[1], joint_in.shape[1]
+    layer_out[...] = layer_in[...]
+    inputs_out[...] = inputs_in[...]
+    inner_out[...] = inner_in[...]
+    outer_out[...] = outer_in[...]
+    joint = joint_in[...]
+    for which, out in enumerate((output_out, query_out, key_out, value_out)):
+        out[...] = joint[:, which * piece : (which + 1) * piece]
+
+    @pl.when(pl.program_id(0) == 0)
+    def _():
+        bias = bias_in[0:1, :]
+        query_bias_out[...] = bias[:, piece : 2 * piece].reshape(piece)
+        value_bias_out[...] = bias[:, 3 * piece :].reshape(piece)
+        for index in range(6):
+            vectors_out[index][...] = shared_in[index : index + 1, :].reshape(width)
+        vectors_out[6][...] = bias_in[1:2, :].reshape(width)
 
 
 def shards(
@@ -725,16 +805,6 @@
     hidden_units = inner_weight.shape[1]
     heads = piece // HEAD_DIM
     assert col_size == 4 and length == 2 * tokens and 4 * piece == width == hidden_units
-    joint = jnp.concatenate([output_weight, query_weight, key_weight, value_weight], axis=1)
-    none = jnp.zeros((piece,), F32)
-    joint_bias = jnp.concatenate([none, query_bias, none, value_bias])
-    own_bias = jnp.zeros((8, width), F32).at[0].set(joint_bias).at[1].set(inner_bias)
-    vectors = jnp.stack(
-        [output_bias, first_gain, first_shift, outer_bias, second_gain, second_shift]
-        + [jnp.zeros_like(output_bias)] * 2
-    )
-    segment = lax.dynamic_index_in_dim(segments, lax.axis_index("col") // 2, 0, keepdims=True)
-    seg_col = segment.reshape(length, 1)
     half = block // 2
     vmem = pl.BlockSpec(memory_space=pltpu.VMEM)
 
@@ -744,6 +814,10 @@
     per_head = pltpu.VMEM((2 * heads, length, HEAD_DIM), BF16)
     weights = pltpu.VMEM((2, width, width), BF16)
     scratch = [
+        pltpu.VMEM((block, width), BF16),
+        pltpu.VMEM((length, 128), F32),
+        pltpu.VMEM((1, length), F32),
+        pltpu.VMEM((8, width), F32),
         weights,
         weights,
         weights,
@@ -785,15 +859,7 @@
         pltpu.SemaphoreType.DMA((256,)),
         pltpu.SemaphoreType.DMA((256,)),
     ]
-    (
-        layer_out,
-        grad_inputs,
-        grad_joint,
-        grad_inner,
-        grad_outer,
-        shared,
-        biases,
-    ) = pl.pallas_call(
+    results = pl.pallas_call(
         functools.partial(layer_kernel, (dp_size, row_size)),
         out_shape=[
             shape((tokens, width), BF16),
@@ -804,7 +870,7 @@
             shape((8, width), F32),
             shape((8, width), F32),
         ],
-        in_specs=[vmem] * 9,
+        in_specs=[vmem] * 18,
         out_specs=[vmem] * 7,
         scratch_shapes=scratch,
         compiler_params=pltpu.CompilerParams(
@@ -812,34 +878,70 @@
         ),
         name="layer",
     )(
-        joint,
+        output_weight,
+        query_weight,
+        key_weight,
+        value_weight,
         inner_weight,
         outer_weight,
         hidden,
         upstream,
-        seg_col,
-        segment,
-        own_bias,
-        vectors,
+        segments,
+        query_bias,
+        value_bias,
+        inner_bias,
+        output_bias,
+        first_gain,
+        first_shift,
+        outer_bias,
+        second_gain,
+        second_shift,
     )
+    steps = 4
+
+    def part(rows, columns):
+        return pl.BlockSpec((rows // steps, columns), lambda i: (i, 0))
+
+    def all_of(rows, columns):
+        return pl.BlockSpec((rows, columns), lambda i: (0, 0))
+
+    big = [part(tokens, width)] * 2
+    small = [part(block, piece)] * 4
+    square = [part(block, width)] * 2
+    outs = pl.pallas_call(
+        unpack_kernel,
+        grid=(steps,),
+        out_shape=[shape((tokens, width), BF16), shape((tokens, width), F32)]
+        + [shape((block, piece), F32)] * 4
+        + [shape((block, width), F32)] * 2
+        + [shape((piece,), F32)] * 2
+        + [shape((width,), F32)] * 7,
+        in_specs=big + [part(block, width)] + square + [all_of(8, width)] * 2,
+        out_specs=big + small + square + [pl.BlockSpec((piece,), lambda i: (0,))] * 2
+        + [pl.BlockSpec((width,), lambda i: (0,))] * 7,
+        name="unpack",
+    )(*results)
+    layer_out, grad_inputs, grad_query, grad_key, grad_value, grad_output = outs[:6]
+    grad_inner, grad_outer = outs[6:8]
+    vectors = outs[8:]
     return (
         layer_out,
         grad_inputs,
-        grad_joint[:, piece : 2 * piece],
-        grad_joint[:, 2 * piece : 3 * piece],
-        grad_joint[:, 3 * piece :],
-        biases[0, piece : 2 * piece],
-        biases[0, 3 * piece :],
-        grad_joint[:, :piece],
-        shared[0],
-        shared[1],
-        shared[2],
+        grad_query,
+        grad_key,
+        grad_value,
+        vectors[0],
+        vectors[1],
+        grad_output,
+        vectors[2],
+        vectors[3],
+        vectors[4],
         grad_inner,
-        biases[1],
+        vectors[8],
         grad_outer,
-        shared[3],
-        shared[4],
-        shared[5],
+        vectors[5],
+        vectors[6],
+        vectors[7],
     )
 
 

time: 240 us -> 223 us (0.929)
  local copies, waits for them, and re-layouts: 19.6 us -> 0 us
  Pallas kernels: 217 us -> 222 us
  other arithmetic: 2.66 us -> 0 us
    another operation x10 -> x0, local copies, waits for them, and re-layouts: 5.48 us -> none  [the longest x8 4.78 us: shards(): jnp.stack([output_bias, first_gain, first_shift, outer_bias, second_gain,...]
    slice x3 -> x0, local copies, waits for them, and re-layouts: 5.15 us -> none  [the longest x1 2.38 us: shards(): grad_joint[:, :piece]]
    pallas_call x0 -> x1, Pallas kernels: none -> 4.96 us  [shards(): pl.pallas_call(unpack_kernel, grid=(steps,), out_shape=[shape((tokens, wi...]
    unnamed x14 -> x0, local copies, waits for them, and re-layouts: 3.97 us -> none
    concatenate x2 -> x0, other arithmetic: 2.66 us -> none  [the longest x1 1.89 us: shards(): jnp.concatenate([output_weight, query_weight, key_weight, value_weight],...]
where the time goes in v2:
time: 223 us
  Pallas kernels  222 us (100%)
    pallas_call x1, Pallas kernels, shards(): pl.pallas_call(functools.partial(layer_kernel, (dp_size, row_size)), out_...  217 us
    pallas_call x1, Pallas kernels, shards(): pl.pallas_call(unpack_kernel, grid=(steps,), out_shape=[shape((tokens, wi...  4.96 us

profile of v2, /device:TPU:0, one launch (start us, length us, event | category | flops | bytes accessed | tf_op | source)
XLA Modules:
  0.0 223.0 jit_solution(2888960425878981840)
XLA Ops:
  0.7 217.2 %layer.1 = (bf16[512,768]{1,0:T(8,128)(2,1)}, f32[512,768]{1,0:T(8,128)}, f32[192,768]{1,0:T(8,128)}, f32[192,768]{1,0:T(8,128)}, f32[192,768]{1,0:T(8,128)}, /*index=5*/f32[8,768]{1,0:T(8,128)}, f32[8,768]{1,0:T(8,128)}) custom-call(bf16[192,192]{1,0:T(8,128)(2,1)} %output_weight.1, bf16[192,192]{1,0:T(8,128)(2,1)} %query_weight.1, ...), custom_call_target="tpu_custom_call" | custom-call | tf_op jit(solution)/shard_map/layer/pallas_call | solution.py:862
  217.8 5.0 %unpack.1 = (bf16[512,768]{1,0:T(8,128)(2,1)}, f32[512,768]{1,0:T(8,128)}, f32[192,192]{1,0:T(8,128)}, f32[192,192]{1,0:T(8,128)}, f32[192,192]{1,0:T(8,128)}, /...) custom-call(bf16[512,768]{1,0:T(8,128)(2,1)} %get-tuple-element.41.l, ...), custom_call_target="tpu_custom_call" | custom-call | tf_op jit(solution)/shard_map/unpack/pallas_call | solution.py:911

commit v3 on v2

--- a/solution.py
+++ b/solution.py
@@ -102,13 +102,19 @@
     outer_bias,
     second_gain,
     second_shift,
+    layer_hbm,
+    inputs_hbm,
+    joint_hbm,
+    inner_hbm,
+    outer_hbm,
+    out_shared,
+    out_bias,
     layer_out,
     grad_inputs,
     out_joint,
     out_inner,
     out_outer,
-    out_shared,
-    out_bias,
+    store_sem,
     own_joint,
     seg_col,
     seg_row,
@@ -175,11 +181,27 @@
     z_peers = [{"dp": dp, "row": flip(row, mask), "col": col} for mask in range(1, row_size)]
     z_of = [flip(row, mask) for mask in range(row_size)]
     copies = Copies(send_sem, recv_sem)
-
-    parts = [output_weight[...], query_weight[...], key_weight[...], value_weight[...]]
-    own_joint[...] = jnp.concatenate(parts, axis=1)
+    pairs = (
+        (layer_out, layer_hbm),
+        (grad_inputs, inputs_hbm),
+        (out_joint, joint_hbm),
+        (out_inner, inner_hbm),
+        (out_outer, outer_hbm),
+    )
+    stores = [
+        pltpu.make_async_copy(src, dst, store_sem.at[i]) for i, (src, dst) in enumerate(pairs)
+    ]
+
+    def by_head(shared, kinds):
+        parts = [shared]
+        for i in range(heads):
+            parts += [kind[:, i * HEAD_DIM : (i + 1) * HEAD_DIM] for kind in kinds]
+        return jnp.concatenate(parts, axis=1)
+
+    kinds = [query_weight[...], key_weight[...], value_weight[...]]
+    own_joint[...] = by_head(output_weight[...], kinds)
     none = jnp.zeros((1, piece), F32)
-    joint_bias = jnp.concatenate([none, row_of(query_bias), none, row_of(value_bias)], axis=1)
+    joint_bias = by_head(none, [row_of(query_bias), none, row_of(value_bias)])
     rest = jnp.zeros((6, width), F32)
     own_bias[...] = jnp.concatenate([joint_bias, row_of(inner_bias), rest], axis=0)
     barrier = pltpu.get_barrier_semaphore()
@@ -197,51 +219,57 @@
         return rows_at(z * block, block)
 
     class Gather:
-        def __init__(self, own, full):
-            self.own, self.full = own, full
+        def __init__(self, own, full, wide):
             source = own.at[rows_at(side * half, half)]
             spot = full.at[mine, half_rows(row, side)]
-            self.z = [copies.new(source, spot, peer) for peer in z_peers]
+            self.z = [copies.new(own, full.at[mine, block_rows(row)], z_peers[0])]
+            self.z += [copies.new(source, spot, peer) for peer in z_peers[1:]]
             self.x_own = copies.new(own, full.at[mine, block_rows(row)], x_peer)
             got = [full.at[mine, half_rows(z, side)] for z in z_of[1:]]
-            self.x = [copies.new(ref, ref, x_peer) for ref in got]
-            self.y = [copies.new(ref, ref, y_peer) for ref in got]
+            self.wide = 1 if wide else 0
+            sent = [full.at[mine, block_rows(z_of[1])] if wide else got[0]] + got[1:]
+            self.x = [copies.new(ref, ref, x_peer) for ref in sent]
+            self.y = [copies.new(ref, ref, y_peer) for ref in got[1:]]
             got = [full.at[other, half_rows(z, side)] for z in z_of[1:]]
-            self.xy = [copies.new(ref, ref, y_peer) for ref in got]
-
-        def start(self):
-            self.z[0].start()
-            self.x_own.start()
-
-        def near(self):
-            self.z[0].wait_recv()
-            self.y[0].start()
-            self.x[0].start()
-            for copy in self.z[1:]:
+            self.xy = [copies.new(ref, ref, y_peer) for ref in got[self.wide :]]
+
+        def start_z(self):
+            for copy in self.z:
                 copy.start()
 
-        def far(self):
-            for z, x, y in list(zip(self.z, self.x, self.y))[1:]:
-                z.wait_recv()
-                y.start()
-                x.start()
+        def wait_z(self):
+            for copy in self.z:
+                copy.wait_recv()
+
+        def start_x(self):
+            for copy in self.x[1:] + self.x[:1]:
+                copy.start()
+
+        def start_y(self):
+            for copy in self.y:
+                copy.start()
+
+        def wait_y(self):
+            for copy in self.y:
+                copy.wait_recv()
 
         def across(self):
-            for x, xy in zip(self.x, self.xy):
+            for x, xy in zip(self.x[self.wide :], self.xy):
                 x.wait_recv()
                 xy.start()
 
         def done(self):
             self.x_own.wait_recv()
-            for copy in self.y + self.xy:
+            for copy in self.x[: self.wide] + self.xy:
                 copy.wait_recv()
 
     gathers = [
-        Gather(own_joint, w_joint),
-        Gather(own_inner, w_inner),
-        Gather(own_outer, w_outer),
+        Gather(own_joint, w_joint, False),
+        Gather(own_inner, w_inner, False),
+        Gather(own_outer, w_outer, True),
     ]
-    gathers[0].start()
+    gathers[0].start_z()
+    gathers[0].x_own.start()
     own_rows_all = rows_at(own_start, tokens)
     send_x = copies.new(hidden, x_full.at[own_rows_all], partner)
     send_x.start()
@@ -256,61 +284,86 @@
     shared_sum[...] = jnp.zeros_like(shared_sum)
     bias_sum[...] = jnp.zeros_like(bias_sum)
 
-    gathers[0].near()
-    gathers[0].far()
-    gathers[1].start()
-    gathers[0].across()
-    gathers[1].near()
+    for index, z_copy in enumerate(gathers[0].z):
+        z_copy.wait_recv()
+        if index:
+            gathers[0].y[index - 1].start()
+        gathers[0].x[index].start()
+    gathers[1].start_z()
     send_x.wait_recv()
     send_bias.wait_recv()
-    gathers[0].done()
-
-    def project(tile, carry):
-        rows = rows_at(tile * TILE, TILE)
-        x = x_full[rows, :]
-        for h in range(2):
-            out = dot(x, w_joint[h, :, 128:], 1, 0) + bias_full[h, 0:1, 128:]
-            at = piece - 128
+    gathers[0].wait_y()
+    gathers[0].across()
+    gathers[1].x_own.start()
+
+    def project(h):
+        def body(tile, carry):
+            rows = rows_at(tile * TILE, TILE)
+            out = dot(x_full[rows, :], w_joint[h, :, 128:], 1, 0) + bias_full[h, 0:1, 128:]
             for which, target in enumerate((query, keys, values)):
                 for i in range(heads):
-                    start = at + which * piece + i * HEAD_DIM
-                    part = out[:, start : start + HEAD_DIM].astype(BF16)
+                    at = piece - 128 + (3 * i + which) * HEAD_DIM
+                    part = out[:, at : at + HEAD_DIM].astype(BF16)
                     if which == 0:
                         part = part * SCALE
                     target[h * heads + i, rows, :] = part.astype(BF16)
+            return carry
+
+        lax.fori_loop(0, tiles, body, 0)
+
+    lanes = lax.broadcasted_iota(jnp.int32, (TILE, 128), 1)
+    half_steps = heads * tiles
+
+    def at_steps(step, services):
+        for when, service in services.items():
+
+            @pl.when(step == when)
+            def _(service=service):
+                service()
+
+    def forward_z():
+        gathers[1].wait_z()
+        gathers[1].start_y()
+        gathers[1].start_x()
+        gathers[2].start_z()
+
+    def forward_across():
+        gathers[1].wait_y()
+        gathers[1].across()
+
+    def forward_last():
+        gathers[2].wait_z()
+        gathers[2].start_x()
+
+    before = {half_steps: gathers[0].done}
+    after = {
+        4: forward_z,
+        half_steps - 1: gathers[2].x_own.start,
+        half_steps + 2: forward_across,
+        half_steps + 5: forward_last,
+        half_steps + 11: gathers[2].start_y,
+    }
+
+    def attend(step, carry):
+        turn = step // half_steps
+        h = mine + (1 - 2 * mine) * turn
+        head = h * heads + lax.rem(step, half_steps) // tiles
+        tile = lax.rem(step, tiles)
+        at_steps(step, before)
+        pl.when(lax.rem(step, half_steps) == 0)(lambda: project(h))
+        rows = rows_at(tile * TILE, TILE)
+        scores = dot(query[head, rows, :], keys[head], 1, 1)
+        scores = jnp.where(seg_col[rows, 0:1] == seg_row[...], scores, NEG_FILL)
+        peak = jnp.max(scores, axis=1, keepdims=True)
+        expos = jnp.exp(scores - peak)
+        total = jnp.sum(expos, axis=1, keepdims=True)
+        out = dot(expos.astype(BF16), values[head], 1, 0) / total
+        head_mixed[head, rows, :] = out.astype(BF16)
+        log_sums[rows, :] = jnp.where(lanes == head, peak + jnp.log(total), log_sums[rows, :])
+        at_steps(step, after)
         return carry
 
-    lax.fori_loop(0, tiles, project, 0)
-    gathers[1].far()
-
-    lanes = lax.broadcasted_iota(jnp.int32, (TILE, 128), 1)
-
-    def attend(head):
-        def body(tile, carry):
-            rows = rows_at(tile * TILE, TILE)
-            scores = dot(query[head, rows, :], keys[head], 1, 1)
-            scores = jnp.where(seg_col[rows, 0:1] == seg_row[...], scores, NEG_FILL)
-            peak = jnp.max(scores, axis=1, keepdims=True)
-            expos = jnp.exp(scores - peak)
-            total = jnp.sum(expos, axis=1, keepdims=True)
-            out = dot(expos.astype(BF16), values[head], 1, 0) / total
-            head_mixed[head, rows, :] = out.astype(BF16)
-            log_sums[rows, :] = jnp.where(lanes == head, peak + jnp.log(total), log_sums[rows, :])
-            return carry
-
-        lax.fori_loop(0, tiles, body, 0)
-
-    services = [
-        gathers[1].across,
-        gathers[2].start,
-        gathers[2].near,
-        lambda: (gathers[1].done(), gathers[2].far()),
-        gathers[2].across,
-        lambda: None,
-    ]
-    for head in range(2 * heads):
-        attend(head)
-        services[min(head, len(services) - 1)]()
+    lax.fori_loop(0, 2 * half_steps, attend, 0)
 
     def join(tile, carry):
         rows = rows_at(tile * TILE, TILE)
@@ -403,8 +456,11 @@
             gelu_slope[h, rows, :] = (below + pre * density).astype(BF16)
         return start
 
+    gathers[1].done()
     lax.fori_loop(0, own_tiles, inner, own_start)
     share_first.wait()
+    gathers[2].wait_y()
+    gathers[2].across()
     lax.fori_loop(0, own_tiles, inner, far_start)
     gathers[2].done()
 
@@ -432,104 +488,104 @@
         add_shared(4, grads * normed)
         add_shared(5, grads)
     share_two.wait()
+    stores[0].start()
 
     class Reduce:
-        def __init__(self, number, grads, out, x_first):
-            self.grads, self.out, self.x_first = grads, out, x_first
-            self.pool = pool = xy_recv.at[number]
-            self.late = late = [rows_at(width + z * half, half) for z in z_of]
-            self.zr, self.fs, self.fr = z_recv.at[number], f_send.at[number], f_recv.at[number]
+        def __init__(self, number, grads, out, lane_set):
+            self.lane_set, self.out = lane_set, out.at[:, lane_set]
+            self.pool, self.zr = xy_recv.at[number, :, lane_set], z_recv.at[number, :, :, lane_set]
+            self.fs, self.fr = f_send.at[number, :, lane_set], f_recv.at[number, :, :, lane_set]
+            self.grads = grads = grads.at[:, :, lane_set]
             away = 1 - side
-            if x_first:
-                self.first = [
-                    copies.new(grads.at[other, block_rows(z)], pool.at[block_rows(z)], x_peer)
-                    for z in z_of
-                ]
-                self.second = [
-                    copies.new(
-                        grads.at[mine, half_rows(z, away)],
-                        pool.at[late[j]],
-                        y_peer,
-                    )
-                    for j, z in enumerate(z_of)
-                ]
-            else:
-                self.first = [
-                    copies.new(
-                        grads.at[h, half_rows(z, away)], pool.at[self.early(h, z)], y_peer
-                    )
-                    for h in (other, mine)
-                    for z in z_of
-                ]
-                self.second = [
-                    copies.new(
-                        grads.at[other, half_rows(z, side)],
-                        pool.at[late[j]],
-                        x_peer,
-                    )
-                    for j, z in enumerate(z_of)
-                ]
-            self.third = [
-                copies.new(
-                    grads.at[mine, half_rows(z, side)],
-                    self.zr.at[mask],
-                    peer,
-                )
-                for mask, (z, peer) in enumerate(zip(z_of[1:], z_peers))
+            self.first, self.first_mine, self.second = [], [], []
+            for j, z in enumerate(z_of):
+                slot = [self.pool.at[pl.ds((3 * j + k) * half, half)] for k in range(3)]
+                if j % 2 == 0:
+                    both = self.pool.at[pl.ds(3 * j * half, block)]
+                    self.first.append(copies.new(grads.at[other, block_rows(z)], both, x_peer))
+                    self.first_mine.append(None)
+                    source = grads.at[mine, half_rows(z, away)]
+                    self.second.append(copies.new(source, slot[2], y_peer))
+                else:
+                    source = grads.at[other, half_rows(z, away)]
+                    self.first.append(copies.new(source, slot[0], y_peer))
+                    source = grads.at[mine, half_rows(z, away)]
+                    self.first_mine.append(copies.new(source, slot[1], y_peer))
+                    source = grads.at[other, half_rows(z, side)]
+                    self.second.append(copies.new(source, slot[2], x_peer))
+            self.third, bit = {}, 1
+            while bit < row_size:
+                for j in range(bit, row_size, 2 * bit):
+                    source = grads.at[mine, half_rows(z_of[j], side)]
+                    slot = self.zr.at[j - 1]
+                    self.third[j] = copies.new(source, slot, z_peers[bit - 1])
+                bit *= 2
+            self.fourth = [copies.new(self.fs, self.fr.at[dp], peer) for peer in dp_peers]
+            self.order = [j for j in range(row_size - 1, -1, -1) if j % 2] + [
+                j for j in range(row_size - 1, -1, -1) if j % 2 == 0
             ]
-            self.fourth = [copies.new(self.fs, self.fr.at[dp], peer) for peer in dp_peers]
-            self.order = list(range(1, row_size)) + [0]
-
-        def early(self, h, z):
-            return rows_at(h * (width // 2) + z * half, half)
-
-        def start(self):
+
+        def start_other(self):
             for j in self.order:
                 self.first[j].start()
 
-        def start_rest(self):
+        def start_mine(self):
             for j in self.order:
-                self.first[row_size + j].start()
-
-        def add(self, rows, h, recv):
-            total = self.grads[h, rows, :].astype(F32) + recv.astype(F32)
+                if j % 2:
+                    self.first_mine[j].start()
+
+        def add(self, h, rows, *slots):
+            total = self.grads[h, rows, :].astype(F32)
+            for start, size in slots:
+                total = total + self.pool[pl.ds(start * half, size), :].astype(F32)
             self.grads[h, rows, :] = total.astype(BF16)
 
-        def go_second(self):
+        def go_second(self, odd):
             for j in self.order:
-                z = z_of[j]
-                self.first[j].wait_recv()
-                if self.x_first:
-                    self.add(block_rows(z), mine, self.pool[block_rows(z), :])
-                else:
-                    self.add(half_rows(z, side), other, self.pool[self.early(other, z), :])
-                self.second[j].start()
+                if j % 2 == odd:
+                    self.first[j].wait_recv()
+                    if odd:
+                        self.add(other, half_rows(z_of[j], side), (3 * j, half))
+                    else:
+                        self.add(mine, block_rows(z_of[j]), (3 * j, block))
+                    self.second[j].start()
 
         def go_third(self):
             for j in self.order:
-                z = z_of[j]
-                rows = half_rows(z, side)
-                if not self.x_first:
-                    self.first[row_size + j].wait_recv()
-                self.second[j].wait_recv()
-                if self.x_first:
-                    self.add(rows, mine, self.pool[self.late[j], :])
+                rows = half_rows(z_of[j], side)
+                if j % 2:
+                    self.first_mine[j].wait_recv()
+                    self.second[j].wait_recv()
+                    self.add(mine, rows, (3 * j + 1, half), (3 * j + 2, half))
                 else:
-                    total = (
-                        self.grads[mine, rows, :].astype(F32)
-                        + self.pool[self.early(mine, z), :].astype(F32)
-                        + self.pool[self.late[j], :].astype(F32)
-                    )
-                    self.grads[mine, rows, :] = total.astype(BF16)
-                if j:
-                    self.third[j - 1].start()
+                    self.second[j].wait_recv()
+                    self.add(mine, rows, (3 * j + 2, half))
+                if j % 2:
+                    self.third[j].start()
+
+        def go_along(self):
+            for j in range(2, row_size, 2):
+                self.take_third(j)
+                self.third[j].start()
+
+        def take_third(self, j):
+            bit = 1
+            while bit < row_size and j % (2 * bit) == 0:
+                self.third[j + bit].wait_recv()
+                bit *= 2
+            rows = half_rows(z_of[j], side)
+            total = self.grads[mine, rows, :].astype(F32)
+            bit = 1
+            while bit < row_size and j % (2 * bit) == 0:
+                total = total + self.zr[j + bit - 1].astype(F32)
+                bit *= 2
+            if j:
+                self.grads[mine, rows, :] = total.astype(BF16)
+            else:
+                self.fs[...] = total.astype(BF16)
 
         def go_fourth(self):
-            total = self.grads[mine, half_rows(row, side), :].astype(F32)
-            for mask, copy in enumerate(self.third):
-                copy.wait_recv()
-                total = total + self.zr[mask].astype(F32)
-            self.fs[...] = total.astype(BF16)
+            self.take_third(0)
             for copy in self.fourth:
                 copy.start()
 
@@ -543,9 +599,12 @@
                     total = total + self.fr[index].astype(F32)
                 self.out[pl.ds(which * half, half), :] = total
 
-    reduce_outer = Reduce(0, g_outer, out_outer, True)
-    reduce_inner = Reduce(1, g_inner, out_inner, False)
-    reduce_joint = Reduce(2, g_joint, out_joint, True)
+    cut = width // 2
+    lane_sets = (pl.ds(0, cut), pl.ds(cut, cut))
+    reduce_outer = Reduce(0, g_outer, out_outer, pl.ds(0, width))
+    reduce_inner = Reduce(1, g_inner, out_inner, pl.ds(0, width))
+    joint_a = Reduce(2, g_joint, out_joint, lane_sets[0])
+    joint_b = Reduce(2, g_joint, out_joint, lane_sets[1])
 
     def weight_grad(target, rows_of, cols_of, h):
         def body(tile, carry):
@@ -556,7 +615,7 @@
         lax.fori_loop(0, width_tiles, body, 0)
 
     weight_grad(g_outer, branch_two, activated, other)
-    reduce_outer.start()
+    reduce_outer.start_other()
 
     def back_inner(tile, carry):
         rows = rows_at(tile * TILE, TILE)
@@ -580,6 +639,7 @@
         copy.wait_send()
     back_one.give()
     weight_grad(g_outer, branch_two, activated, mine)
+    reduce_outer.start_mine()
     share_one = Share(branch_one)
     for i in range(own_tiles):
         rows = pl.ds(i * TILE, TILE)
@@ -595,9 +655,9 @@
     send_shared = copies.new(shared_sum, shared_pair, partner)
     send_shared.start()
     weight_grad(g_inner, first_rows, gelu_slope, other)
-    reduce_inner.start()
+    reduce_inner.start_other()
     weight_grad(g_inner, first_rows, gelu_slope, mine)
-    reduce_inner.start_rest()
+    reduce_inner.start_mine()
     share_one.wait()
 
     def back_mixed(tile, carry):
@@ -611,77 +671,95 @@
         return carry
 
     lax.fori_loop(0, tiles, back_mixed, 0)
-    reduce_outer.go_second()
-
-    def attend_back(head, carry):
+    reduce_outer.go_second(0)
+    reduce_outer.go_second(1)
+
+    def back_setup(head):
         q_turned[...] = query[head].T
         o_turned[...] = grad_heads[head].T
         dk_turned[...] = jnp.zeros_like(dk_turned)
         dv_turned[...] = jnp.zeros_like(dv_turned)
 
+    def back_finish(head):
+        keys[head] = dk_turned[...].T.astype(BF16)
+        values[head] = dv_turned[...].T.astype(BF16)
+
+    grad_rows = activated
+
+    members = ([0], list(range(1, heads)))
+
+    def gather_heads(h, which):
+        lane_set = lane_sets[which]
+
         def body(tile, carry):
             rows = rows_at(tile * TILE, TILE)
-            q, g = query[head, rows, :], grad_heads[head, rows, :]
-            scores = dot(q, keys[head], 1, 1)
-            scores = jnp.where(seg_col[rows, 0:1] == seg_row[...], scores, NEG_FILL)
-            log_sum = jnp.sum(
-                jnp.where(lanes == head, log_sums[rows, :], 0.0), axis=1, keepdims=True
-            )
-            probs = jnp.exp(scores - log_sum)
-            grad_probs = dot(g, values[head], 1, 1)
-            inner_sum = jnp.sum(
-                g.astype(F32) * head_mixed[head, rows, :].astype(F32), axis=1, keepdims=True
-            )
-            grad_scores = (probs * (grad_probs - inner_sum)).astype(BF16)
-            dv_turned[...] += dot(o_turned[:, rows], probs.astype(BF16), 1, 0)
-            dk_turned[...] += dot(q_turned[:, rows], grad_scores, 1, 0)
-            query[head, rows, :] = (dot(grad_scores, keys[head], 1, 0) * SCALE).astype(BF16)
-            return carry
-
-        lax.fori_loop(0, tiles, body, 0)
-        keys[head] = dk_turned[...].T.astype(BF16)
-        values[head] = dv_turned[...].T.astype(BF16)
-        return carry
-
-    grad_rows = activated
-
-    def gather_heads(h):
-        def body(tile, carry):
-            rows = rows_at(tile * TILE, TILE)
-            parts = [jnp.zeros((TILE, piece), BF16)]
-            for source in (query, keys, values):
-                for i in range(heads):
-                    parts.append(source[h * heads + i, rows, :])
+            parts = [] if which else [jnp.zeros((TILE, piece), BF16)]
+            for i in members[which]:
+                parts += [source[h * heads + i, rows, :] for source in (query, keys, values)]
             joined = jnp.concatenate(parts, axis=1)
-            grad_rows[h, rows, :] = joined
-            bias_sum[h, 0:1, :] += jnp.sum(joined.astype(F32), axis=0, keepdims=True)
+            grad_rows[h, rows, lane_set] = joined
+            bias_sum[h, 0:1, lane_set] += jnp.sum(joined.astype(F32), axis=0, keepdims=True)
             return carry
 
         lax.fori_loop(0, tiles, body, 0)
 
         def joint_grad(tile, carry):
             at = pl.ds(pl.multiple_of(tile * TILE, TILE), TILE)
-            g_joint[h, at, :] = dot(x_full[:, at], grad_rows[h], 0, 0).astype(BF16)
-            g_joint[h, at, :piece] = dot(branch_one[:, at], mixed[h], 0, 0).astype(BF16)
+            g_joint[h, at, lane_set] = dot(x_full[:, at], grad_rows[h, :, lane_set], 0, 0).astype(
+                BF16
+            )
+            if which == 0:
+                g_joint[h, at, :piece] = dot(branch_one[:, at], mixed[h], 0, 0).astype(BF16)
             return carry
 
         lax.fori_loop(0, width_tiles, joint_grad, 0)
 
-    attend_back(other * heads, 0)
-    reduce_outer.go_third()
-    attend_back(other * heads + 1, 0)
-    reduce_inner.go_second()
-    lax.fori_loop(other * heads + 2, other * heads + heads, attend_back, 0)
-    gather_heads(other)
-    reduce_joint.start()
-    reduce_outer.go_fourth()
-    attend_back(mine * heads, 0)
-    reduce_inner.go_third()
-    attend_back(mine * heads + 1, 0)
-    reduce_inner.go_fourth()
-    reduce_outer.done()
-    lax.fori_loop(mine * heads + 2, mine * heads + heads, attend_back, 0)
-    gather_heads(mine)
+    after_back = {
+        6: joint_a.start_other,
+        8: lambda: reduce_inner.go_second(0),
+        9: lambda: reduce_inner.go_second(1),
+        11: lambda: (reduce_outer.go_third(), joint_b.start_other()),
+        15: joint_a.start_mine,
+        16: reduce_outer.go_along,
+        18: lambda: joint_a.go_second(1),
+        19: lambda: joint_a.go_second(0),
+        20: reduce_inner.go_third,
+        21: lambda: joint_b.go_second(1),
+        22: reduce_outer.go_fourth,
+    }
+
+    def attend_back(step, carry):
+        turn = step // half_steps
+        h = other + (1 - 2 * other) * turn
+        head = h * heads + lax.rem(step, half_steps) // tiles
+        tile = lax.rem(step, tiles)
+        pl.when(tile == 0)(lambda: back_setup(head))
+        rows = rows_at(tile * TILE, TILE)
+        q, g = query[head, rows, :], grad_heads[head, rows, :]
+        scores = dot(q, keys[head], 1, 1)
+        scores = jnp.where(seg_col[rows, 0:1] == seg_row[...], scores, NEG_FILL)
+        log_sum = jnp.sum(jnp.where(lanes == head, log_sums[rows, :], 0.0), axis=1, keepdims=True)
+        probs = jnp.exp(scores - log_sum)
+        grad_probs = dot(g, values[head], 1, 1)
+        inner_sum = jnp.sum(
+            g.astype(F32) * head_mixed[head, rows, :].astype(F32), axis=1, keepdims=True
+        )
+        grad_scores = (probs * (grad_probs - inner_sum)).astype(BF16)
+        dv_turned[...] += dot(o_turned[:, rows], probs.astype(BF16), 1, 0)
+        dk_turned[...] += dot(q_turned[:, rows], grad_scores, 1, 0)
+        query[head, rows, :] = (dot(grad_scores, keys[head], 1, 0) * SCALE).astype(BF16)
+        pl.when(tile == tiles - 1)(lambda: back_finish(head))
+        in_half = lax.rem(step, half_steps)
+        pl.when(in_half == tiles - 1)(lambda: gather_heads(h, 0))
+        pl.when(in_half == half_steps - 1)(lambda: gather_heads(h, 1))
+        at_steps(step, after_back)
+        return carry
+
+    lax.fori_loop(0, 2 * half_steps, attend_back, 0)
+    joint_b.start_mine()
+    joint_b.go_second(0)
+    joint_a.go_third()
+    reduce_inner.go_along()
 
     send_shared.wait_recv()
     vec_x_send, vec_x_recv = vec_x.at[0], vec_x.at[1]
@@ -690,8 +768,6 @@
     send_vec_x = copies.new(vec_x_send, vec_x_recv, x_peer)
     send_vec_x.start()
 
-    reduce_joint.go_second()
-
     def input_partial(rows):
         return dot(grad_rows[0, rows, :], w_joint[0], 1, 1) + dot(
             grad_rows[1, rows, :], w_joint[1], 1, 1
@@ -701,6 +777,15 @@
     for copy in leave_two.copies:
         copy.wait_send()
     back_two.give()
+    for i in range(own_tiles):
+        rows = pl.ds(i * TILE, TILE)
+        grad_inputs[rows, :] = back_two.take(i) + grad_second[rows, :]
+    stores[1].start()
+    joint_a.go_along()
+    joint_b.go_third()
+    reduce_inner.go_fourth()
+    reduce_outer.done()
+    stores[4].start()
 
     send_vec_x.wait_recv()
     vec_dp[dp, :8, :] = vec_x[0, :8, :] + vec_x[1, :8, :]
@@ -708,13 +793,8 @@
     send_vec_dp = [copies.new(vec_dp.at[dp], vec_dp.at[dp], peer) for peer in dp_peers]
     for copy in send_vec_dp:
         copy.start()
-
-    reduce_inner.done()
-    reduce_joint.go_third()
-    for i in range(own_tiles):
-        rows = pl.ds(i * TILE, TILE)
-        grad_inputs[rows, :] = back_two.take(i) + grad_second[rows, :]
-
+    joint_a.go_fourth()
+    joint_b.go_along()
     for copy in send_vec_dp:
         copy.wait_recv()
     total = vec_dp[0]
@@ -724,8 +804,10 @@
     send_vec_z = [copies.new(vec_z.at[row], vec_z.at[row], peer) for peer in z_peers]
     for copy in send_vec_z:
         copy.start()
-
-    reduce_joint.go_fourth()
+    reduce_inner.done()
+    stores[3].start()
+    joint_a.done()
+    joint_b.go_fourth()
     for copy in send_vec_z:
         copy.wait_recv()
     total = vec_z[0]
@@ -733,8 +815,10 @@
         total = total + vec_z[index]
     out_shared[...] = total[:8]
     out_bias[...] = total[8:]
-    reduce_joint.done()
-
+    joint_b.done()
+    stores[2].start()
+    for store in stores:
+        store.wait()
     copies.finish()
 
 
@@ -764,14 +848,21 @@
     inner_out[...] = inner_in[...]
     outer_out[...] = outer_in[...]
     joint = joint_in[...]
-    for which, out in enumerate((output_out, query_out, key_out, value_out)):
-        out[...] = joint[:, which * piece : (which + 1) * piece]
+
+
+    def of_kind(rows, which):
+        starts = range(piece + which * HEAD_DIM, rows.shape[1], 3 * HEAD_DIM)
+        return jnp.concatenate([rows[:, at : at + HEAD_DIM] for at in starts], axis=1)
+
+    output_out[...] = joint[:, :piece]
+    for which, out in enumerate((query_out, key_out, value_out)):
+        out[...] = of_kind(joint, which)
 
     @pl.when(pl.program_id(0) == 0)
     def _():
         bias = bias_in[0:1, :]
-        query_bias_out[...] = bias[:, piece : 2 * piece].reshape(piece)
-        value_bias_out[...] = bias[:, 3 * piece :].reshape(piece)
+        query_bias_out[...] = of_kind(bias, 0).reshape(piece)
+        value_bias_out[...] = of_kind(bias, 2).reshape(piece)
         for index in range(6):
             vectors_out[index][...] = shared_in[index : index + 1, :].reshape(width)
         vectors_out[6][...] = bias_in[1:2, :].reshape(width)
@@ -814,6 +905,12 @@
     per_head = pltpu.VMEM((2 * heads, length, HEAD_DIM), BF16)
     weights = pltpu.VMEM((2, width, width), BF16)
     scratch = [
+        pltpu.VMEM((tokens, width), BF16),
+        pltpu.VMEM((tokens, width), F32),
+        pltpu.VMEM((block, width), F32),
+        pltpu.VMEM((block, width), F32),
+        pltpu.VMEM((block, width), F32),
+        pltpu.SemaphoreType.DMA((5,)),
         pltpu.VMEM((block, width), BF16),
         pltpu.VMEM((length, 128), F32),
         pltpu.VMEM((1, length), F32),
@@ -871,7 +968,7 @@
             shape((8, width), F32),
         ],
         in_specs=[vmem] * 18,
-        out_specs=[vmem] * 7,
+        out_specs=[pl.BlockSpec(memory_space=pl.ANY)] * 5 + [vmem] * 2,
         scratch_shapes=scratch,
         compiler_params=pltpu.CompilerParams(
             collective_id=0, has_side_effects=True, vmem_limit_bytes=67043328

time: 223 us -> 168 us (0.75)
  Pallas kernels: 222 us -> 167 us
    pallas_call x1, Pallas kernels: 217 us -> 162 us  [shards(): pl.pallas_call(functools.partial(layer_kernel, (dp_size, row_size)), out_...]
where the time goes in v3:
time: 168 us
  Pallas kernels  167 us (99%)
    pallas_call x1, Pallas kernels, shards(): pl.pallas_call(functools.partial(layer_kernel, (dp_size, row_size)), out_...  162 us
    pallas_call x1, Pallas kernels, shards(): pl.pallas_call(unpack_kernel, grid=(steps,), out_shape=[shape((tokens, wi...  4.98 us

profile of v3, /device:TPU:0, one launch (start us, length us, event | category | flops | bytes accessed | tf_op | source)
XLA Modules:
  0.0 168.0 jit_solution(11774869179168574289)
XLA Ops:
  0.7 162.2 %layer.1 = (bf16[512,768]{1,0:T(8,128)(2,1)}, f32[512,768]{1,0:T(8,128)}, f32[192,768]{1,0:T(8,128)}, f32[192,768]{1,0:T(8,128)}, f32[192,768]{1,0:T(8,128)}, /*index=5*/f32[8,768]{1,0:T(8,128)}, f32[8,768]{1,0:T(8,128)}) custom-call(bf16[192,192]{1,0:T(8,128)(2,1)} %output_weight.1, bf16[192,192]{1,0:T(8,128)(2,1)} %query_weight.1, ...), custom_call_target="tpu_custom_call" | custom-call | tf_op jit(solution)/shard_map/layer/pallas_call | solution.py:959
  162.8 5.0 %unpack.1 = (bf16[512,768]{1,0:T(8,128)(2,1)}, f32[512,768]{1,0:T(8,128)}, f32[192,192]{1,0:T(8,128)}, f32[192,192]{1,0:T(8,128)}, f32[192,192]{1,0:T(8,128)}, /...) custom-call(bf16[512,768]{1,0:T(8,128)(2,1)} %get-tuple-element.41.l, ...), custom_call_target="tpu_custom_call" | custom-call | tf_op jit(solution)/shard_map/unpack/pallas_call | solution.py:1008

commit v4 on v3

--- a/solution.py
+++ b/solution.py
@@ -132,7 +132,7 @@
     bias_full,
     first_normed,
     first_scale,
-    first_rows,
+    x_turned,
     activated,
     gelu_slope,
     branch_two,
@@ -162,6 +162,7 @@
 ):
     dp_size, row_size = sizes
     grad_second = grad_inputs
+    first_rows = x_full
     tokens, width = hidden.shape
     length = 2 * tokens
     block = own_joint.shape[0]
@@ -220,10 +221,18 @@
 
     class Gather:
         def __init__(self, own, full, wide):
-            source = own.at[rows_at(side * half, half)]
-            spot = full.at[mine, half_rows(row, side)]
-            self.z = [copies.new(own, full.at[mine, block_rows(row)], z_peers[0])]
-            self.z += [copies.new(source, spot, peer) for peer in z_peers[1:]]
+            self.z = {}
+            for j in range(1, row_size):
+                bit = j & -j
+                if j == 1:
+                    source, spot = own, full.at[mine, block_rows(row)]
+                elif j == bit:
+                    source = own.at[rows_at(side * half, half)]
+                    spot = full.at[mine, half_rows(row, side)]
+                else:
+                    source = spot = full.at[mine, half_rows(z_of[j - bit], side)]
+                self.z[j] = copies.new(source, spot, z_peers[bit - 1])
+            self.z_order = sorted(self.z, key=lambda j: (bin(j).count("1"), -j))
             self.x_own = copies.new(own, full.at[mine, block_rows(row)], x_peer)
             got = [full.at[mine, half_rows(z, side)] for z in z_of[1:]]
             self.wide = 1 if wide else 0
@@ -234,12 +243,26 @@
             self.xy = [copies.new(ref, ref, y_peer) for ref in got[self.wide :]]
 
         def start_z(self):
-            for copy in self.z:
-                copy.start()
+            for j in self.z_order:
+                if j & (j - 1) == 0:
+                    self.z[j].start()
+
+        def pass_z(self, j):
+            self.z[j].wait_recv()
+            bit = 1
+            while bit < (j & -j):
+                self.z[j + bit].start()
+                bit *= 2
+
+        def middle_z(self):
+            for j in self.z_order:
+                if j & 1 == 0:
+                    self.pass_z(j)
 
         def wait_z(self):
-            for copy in self.z:
-                copy.wait_recv()
+            for j in self.z_order:
+                if j & 1:
+                    self.z[j].wait_recv()
 
         def start_x(self):
             for copy in self.x[1:] + self.x[:1]:
@@ -284,14 +307,22 @@
     shared_sum[...] = jnp.zeros_like(shared_sum)
     bias_sum[...] = jnp.zeros_like(bias_sum)
 
-    for index, z_copy in enumerate(gathers[0].z):
-        z_copy.wait_recv()
-        if index:
-            gathers[0].y[index - 1].start()
-        gathers[0].x[index].start()
+    first = gathers[0]
+    for j in first.z_order:
+        first.pass_z(j)
+        if j > 1:
+            first.y[j - 2].start()
+        first.x[j - 1].start()
     gathers[1].start_z()
     send_x.wait_recv()
     send_bias.wait_recv()
+
+    def turn(tile, carry):
+        rows = pl.ds(pl.multiple_of(tile * TILE, TILE), TILE)
+        x_turned[:, rows] = x_full[rows, :].T
+        return carry
+
+    lax.fori_loop(0, tiles, turn, 0)
     gathers[0].wait_y()
     gathers[0].across()
     gathers[1].x_own.start()
@@ -337,10 +368,12 @@
 
     before = {half_steps: gathers[0].done}
     after = {
-        4: forward_z,
-        half_steps - 1: gathers[2].x_own.start,
-        half_steps + 2: forward_across,
-        half_steps + 5: forward_last,
+        1: gathers[1].middle_z,
+        6: forward_z,
+        9: gathers[2].x_own.start,
+        half_steps + 1: gathers[2].middle_z,
+        half_steps + 4: forward_across,
+        half_steps + 7: forward_last,
         half_steps + 11: gathers[2].start_y,
     }
 
@@ -597,14 +630,15 @@
                 total = self.fr[which].astype(F32)
                 for index in range(which + 2, dp_size, 2):
                     total = total + self.fr[index].astype(F32)
-                self.out[pl.ds(which * half, half), :] = total
-
-    cut = width // 2
-    lane_sets = (pl.ds(0, cut), pl.ds(cut, cut))
+                self.out[pl.ds(which * half, half), :] = total.astype(BF16)
+
+    cut = width // 6
+    lane_sets = (pl.ds(0, 3 * cut), pl.ds(3 * cut, cut), pl.ds(4 * cut, 2 * cut))
     reduce_outer = Reduce(0, g_outer, out_outer, pl.ds(0, width))
     reduce_inner = Reduce(1, g_inner, out_inner, pl.ds(0, width))
     joint_a = Reduce(2, g_joint, out_joint, lane_sets[0])
     joint_b = Reduce(2, g_joint, out_joint, lane_sets[1])
+    joint_c = Reduce(2, g_joint, out_joint, lane_sets[2])
 
     def weight_grad(target, rows_of, cols_of, h):
         def body(tile, carry):
@@ -686,7 +720,9 @@
 
     grad_rows = activated
 
-    members = ([0], list(range(1, heads)))
+    kinds = (query, keys, values)
+    order = [(i, kind) for i in range(heads) for kind in range(3)]
+    members = (order[:3], order[3:5], order[5:])
 
     def gather_heads(h, which):
         lane_set = lane_sets[which]
@@ -694,8 +730,8 @@
         def body(tile, carry):
             rows = rows_at(tile * TILE, TILE)
             parts = [] if which else [jnp.zeros((TILE, piece), BF16)]
-            for i in members[which]:
-                parts += [source[h * heads + i, rows, :] for source in (query, keys, values)]
+            for i, kind in members[which]:
+                parts.append(kinds[kind][h * heads + i, rows, :])
             joined = jnp.concatenate(parts, axis=1)
             grad_rows[h, rows, lane_set] = joined
             bias_sum[h, 0:1, lane_set] += jnp.sum(joined.astype(F32), axis=0, keepdims=True)
@@ -705,7 +741,7 @@
 
         def joint_grad(tile, carry):
             at = pl.ds(pl.multiple_of(tile * TILE, TILE), TILE)
-            g_joint[h, at, lane_set] = dot(x_full[:, at], grad_rows[h, :, lane_set], 0, 0).astype(
+            g_joint[h, at, lane_set] = dot(x_turned[at, :], grad_rows[h, :, lane_set], 1, 0).astype(
                 BF16
             )
             if which == 0:
@@ -714,17 +750,31 @@
 
         lax.fori_loop(0, width_tiles, joint_grad, 0)
 
+    def start_others():
+        joint_b.start_other()
+        joint_c.start_other()
+
+    def second_bc():
+        joint_b.go_second(1)
+        joint_c.go_second(1)
+
+    def start_middle():
+        joint_b.start_mine()
+        joint_b.go_second(0)
+
     after_back = {
         6: joint_a.start_other,
         8: lambda: reduce_inner.go_second(0),
         9: lambda: reduce_inner.go_second(1),
-        11: lambda: (reduce_outer.go_third(), joint_b.start_other()),
+        11: start_others,
+        12: reduce_outer.go_third,
         15: joint_a.start_mine,
         16: reduce_outer.go_along,
-        18: lambda: joint_a.go_second(1),
-        19: lambda: joint_a.go_second(0),
+        17: lambda: joint_a.go_second(1),
+        18: lambda: joint_a.go_second(0),
+        19: start_middle,
         20: reduce_inner.go_third,
-        21: lambda: joint_b.go_second(1),
+        21: second_bc,
         22: reduce_outer.go_fourth,
     }
 
@@ -751,13 +801,14 @@
         pl.when(tile == tiles - 1)(lambda: back_finish(head))
         in_half = lax.rem(step, half_steps)
         pl.when(in_half == tiles - 1)(lambda: gather_heads(h, 0))
-        pl.when(in_half == half_steps - 1)(lambda: gather_heads(h, 1))
+        pl.when(in_half == 2 * tiles - 1)(lambda: gather_heads(h, 1))
+        pl.when(in_half == half_steps - 1)(lambda: gather_heads(h, 2))
         at_steps(step, after_back)
         return carry
 
     lax.fori_loop(0, 2 * half_steps, attend_back, 0)
-    joint_b.start_mine()
-    joint_b.go_second(0)
+    joint_c.start_mine()
+    joint_c.go_second(0)
     joint_a.go_third()
     reduce_inner.go_along()
 
@@ -777,24 +828,23 @@
     for copy in leave_two.copies:
         copy.wait_send()
     back_two.give()
-    for i in range(own_tiles):
-        rows = pl.ds(i * TILE, TILE)
-        grad_inputs[rows, :] = back_two.take(i) + grad_second[rows, :]
-    stores[1].start()
-    joint_a.go_along()
-    joint_b.go_third()
-    reduce_inner.go_fourth()
-    reduce_outer.done()
-    stores[4].start()
-
     send_vec_x.wait_recv()
     vec_dp[dp, :8, :] = vec_x[0, :8, :] + vec_x[1, :8, :]
     vec_dp[dp, 8:, :] = bias_sum[mine] + vec_x[1, 8:, :]
     send_vec_dp = [copies.new(vec_dp.at[dp], vec_dp.at[dp], peer) for peer in dp_peers]
     for copy in send_vec_dp:
         copy.start()
-    joint_a.go_fourth()
-    joint_b.go_along()
+    for i in range(own_tiles):
+        rows = pl.ds(i * TILE, TILE)
+        grad_inputs[rows, :] = back_two.take(i) + grad_second[rows, :]
+    stores[1].start()
+    joint_b.go_third()
+    joint_a.go_along()
+    joint_c.go_third()
+    reduce_inner.go_fourth()
+    reduce_outer.done()
+    stores[4].start()
+
     for copy in send_vec_dp:
         copy.wait_recv()
     total = vec_dp[0]
@@ -804,10 +854,15 @@
     send_vec_z = [copies.new(vec_z.at[row], vec_z.at[row], peer) for peer in z_peers]
     for copy in send_vec_z:
         copy.start()
+    joint_b.go_along()
+    joint_c.go_along()
+    joint_a.go_fourth()
     reduce_inner.done()
     stores[3].start()
+    joint_b.go_fourth()
+    joint_c.go_fourth()
     joint_a.done()
-    joint_b.go_fourth()
+    joint_b.done()
     for copy in send_vec_z:
         copy.wait_recv()
     total = vec_z[0]
@@ -815,11 +870,12 @@
         total = total + vec_z[index]
     out_shared[...] = total[:8]
     out_bias[...] = total[8:]
-    joint_b.done()
+    joint_c.done()
     stores[2].start()
     for store in stores:
         store.wait()
     copies.finish()
+    assert len(copies.made) == send_sem.shape[0]
 
 
 def unpack_kernel(
@@ -845,9 +901,9 @@
     piece, width = query_out.shape[1], joint_in.shape[1]
     layer_out[...] = layer_in[...]
     inputs_out[...] = inputs_in[...]
-    inner_out[...] = inner_in[...]
-    outer_out[...] = outer_in[...]
-    joint = joint_in[...]
+    inner_out[...] = inner_in[...].astype(F32)
+    outer_out[...] = outer_in[...].astype(F32)
+    joint = joint_in[...].astype(F32)
 
 
     def of_kind(rows, which):
@@ -896,6 +952,11 @@
     hidden_units = inner_weight.shape[1]
     heads = piece // HEAD_DIM
     assert col_size == 4 and length == 2 * tokens and 4 * piece == width == hidden_units
+    copies_of_gather = 3 * (4 * row_size - 4) - 1
+    copies_of_sums = 2 * row_size + row_size // 2 + row_size - 1 + dp_size - 1
+    copies_of_vectors = 2 + dp_size - 1 + row_size - 1
+    copy_count = 2 + copies_of_gather + 7 * (tokens // TILE) + 5 * copies_of_sums
+    copy_count += copies_of_vectors
     half = block // 2
     vmem = pl.BlockSpec(memory_space=pltpu.VMEM)
 
@@ -907,9 +968,9 @@
     scratch = [
         pltpu.VMEM((tokens, width), BF16),
         pltpu.VMEM((tokens, width), F32),
-        pltpu.VMEM((block, width), F32),
-        pltpu.VMEM((block, width), F32),
-        pltpu.VMEM((block, width), F32),
+        pltpu.VMEM((block, width), BF16),
+        pltpu.VMEM((block, width), BF16),
+        pltpu.VMEM((block, width), BF16),
         pltpu.SemaphoreType.DMA((5,)),
         pltpu.VMEM((block, width), BF16),
         pltpu.VMEM((length, 128), F32),
@@ -928,7 +989,7 @@
         pltpu.VMEM((2, 8, width), F32),
         pltpu.VMEM((tokens, width), F32),
         pltpu.VMEM((tokens, 1), F32),
-        pltpu.VMEM((length, width), BF16),
+        pltpu.VMEM((width, length), BF16),
         pltpu.VMEM((2, length, width), BF16),
         pltpu.VMEM((2, length, width), BF16),
         pltpu.VMEM((length, width), BF16),
@@ -953,17 +1014,17 @@
         pltpu.VMEM((2, 16, width), F32),
         pltpu.VMEM((dp_size, 16, width), F32),
         pltpu.VMEM((row_size, 16, width), F32),
-        pltpu.SemaphoreType.DMA((256,)),
-        pltpu.SemaphoreType.DMA((256,)),
+        pltpu.SemaphoreType.DMA((copy_count,)),
+        pltpu.SemaphoreType.DMA((copy_count,)),
     ]
     results = pl.pallas_call(
         functools.partial(layer_kernel, (dp_size, row_size)),
         out_shape=[
             shape((tokens, width), BF16),
             shape((tokens, width), F32),
-            shape((block, width), F32),
-            shape((block, width), F32),
-            shape((block, width), F32),
+            shape((block, width), BF16),
+            shape((block, width), BF16),
+            shape((block, width), BF16),
             shape((8, width), F32),
             shape((8, width), F32),
         ],
@@ -994,7 +1055,7 @@
         second_gain,
         second_shift,
     )
-    steps = 4
+    steps = 2
 
     def part(rows, columns):
         return pl.BlockSpec((rows // steps, columns), lambda i: (i, 0))

time: 168 us -> 167 us (level)
  no operation moved by 1% of the time
where the time goes in v4:
time: 167 us
  Pallas kernels  166 us (99%)
    pallas_call x1, Pallas kernels, shards(): pl.pallas_call(functools.partial(layer_kernel, (dp_size, row_size)), out_...  162 us
    pallas_call x1, Pallas kernels, shards(): pl.pallas_call(unpack_kernel, grid=(steps,), out_shape=[shape((tokens, wi...  3.93 us

profile of v4, /device:TPU:0, one launch (start us, length us, event | category | flops | bytes accessed | tf_op | source)
XLA Modules:
  0.0 166.8 jit_solution(18433670918941398560)
XLA Ops:
  0.7 162.0 %layer.1 = (bf16[512,768]{1,0:T(8,128)(2,1)}, f32[512,768]{1,0:T(8,128)}, bf16[192,768]{1,0:T(8,128)(2,1)}, bf16[192,768]{1,0:T(8,128)(2,1)}, bf16[192,768]{1,0:...) custom-call(bf16[192,192]{1,0:T(8,128)(2,1)} %output_weight.1, bf16[192,192]{1,0:T(8,128)(2,1)} %query_weight.1, ...), custom_call_target="tpu_custom_call" | custom-call | tf_op jit(solution)/shard_map/layer/pallas_call | solution.py:1020
  162.7 3.9 %unpack.1 = (bf16[512,768]{1,0:T(8,128)(2,1)}, f32[512,768]{1,0:T(8,128)}, f32[192,192]{1,0:T(8,128)}, f32[192,192]{1,0:T(8,128)}, f32[192,192]{1,0:T(8,128)}, /...) custom-call(bf16[512,768]{1,0:T(8,128)(2,1)} %get-tuple-element.41.l, ...), custom_call_target="tpu_custom_call" | custom-call | tf_op jit(solution)/shard_map/unpack/pallas_call | solution.py:1069

commit v5 on v4

--- a/solution.py
+++ b/solution.py
@@ -370,9 +370,9 @@
     after = {
         1: gathers[1].middle_z,
         6: forward_z,
-        9: gathers[2].x_own.start,
         half_steps + 1: gathers[2].middle_z,
-        half_steps + 4: forward_across,
+        half_steps + 3: forward_across,
+        half_steps + 4: gathers[2].x_own.start,
         half_steps + 7: forward_last,
         half_steps + 11: gathers[2].start_y,
     }

time: 167 us -> 166 us (level)
  no operation moved by 1% of the time
where the time goes in v5:
time: 166 us
  Pallas kernels  165 us (99%)
    pallas_call x1, Pallas kernels, shards(): pl.pallas_call(functools.partial(layer_kernel, (dp_size, row_size)), out_...  161 us
    pallas_call x1, Pallas kernels, shards(): pl.pallas_call(unpack_kernel, grid=(steps,), out_shape=[shape((tokens, wi...  3.93 us

profile of v5, /device:TPU:0, one launch (start us, length us, event | category | flops | bytes accessed | tf_op | source)
XLA Modules:
  0.0 165.8 jit_solution(656131525269120488)
XLA Ops:
  0.7 161.1 %layer.1 = (bf16[512,768]{1,0:T(8,128)(2,1)}, f32[512,768]{1,0:T(8,128)}, bf16[192,768]{1,0:T(8,128)(2,1)}, bf16[192,768]{1,0:T(8,128)(2,1)}, bf16[192,768]{1,0:...) custom-call(bf16[192,192]{1,0:T(8,128)(2,1)} %output_weight.1, bf16[192,192]{1,0:T(8,128)(2,1)} %query_weight.1, ...), custom_call_target="tpu_custom_call" | custom-call | tf_op jit(solution)/shard_map/layer/pallas_call | solution.py:1020
  161.7 3.9 %unpack.1 = (bf16[512,768]{1,0:T(8,128)(2,1)}, f32[512,768]{1,0:T(8,128)}, f32[192,192]{1,0:T(8,128)}, f32[192,192]{1,0:T(8,128)}, f32[192,192]{1,0:T(8,128)}, /...) custom-call(bf16[512,768]{1,0:T(8,128)(2,1)} %get-tuple-element.41.l, ...), custom_call_target="tpu_custom_call" | custom-call | tf_op jit(solution)/shard_map/unpack/pallas_call | solution.py:1069
